TPU v7x, 32 devices: a whole 2x2x4 slice. The times are simulated.
32 devices in a mesh: dom: 8 (over z, x), sub: 4 (over y, core).
Axes of the slice: x: 2, y: 2, z: 4, core: 2. Of those that a mesh axis runs over, the one named last changes fastest.
Arguments:
- primitive: float32 [5, 65536], P(None, ('dom', 'sub')), may hold values from -3 to 3
- gradient: float32 [15, 65536], P(None, ('dom', 'sub')), may hold values from -1.5 to 1.5
- volume: float32 [65536], P(('dom', 'sub')), may hold values from 0.5 to 4
- face_left: int32 [196608], P(('dom', 'sub')), may hold values from 0 to 2047
- face_right: int32 [196608], P(('dom', 'sub')), may hold values from 0 to 4095, as said below
- face_angles: float32 [2, 196608], P(None, ('dom', 'sub')), may hold values from -3.140625 to 3.140625
- face_area: float32 [196608], P(('dom', 'sub')), may hold values from 0.2 to 2
- face_offsets: float32 [6, 196608], P(None, ('dom', 'sub')), may hold values from -1 to 1
- rim_left: int32 [16384], P(('dom', 'sub')), may hold values from 0 to 511
- rim_right: int32 [16384], P(('dom', 'sub')), may hold values from 0 to 511
- rim_angles: float32 [2, 16384], P(None, ('dom', 'sub')), may hold values from -3.140625 to 3.140625
- rim_area: float32 [16384], P(('dom', 'sub')), may hold values from 0.2 to 2
- rim_offsets: float32 [6, 16384], P(None, ('dom', 'sub')), may hold values from -1 to 1
- send_list: int32 [512], P(('dom', 'sub')), may hold values from -1 to 15, as said below
Outputs:
- change_rate: float32 [5, 65536], P(None, ('dom', 'sub'))
- new_conserved: float32 [5, 65536], P(None, ('dom', 'sub'))
- time_step: float32 [], replicated
Inputs may be any that keep to these rules, and one draw needn't show every extreme that they name: `send_list`: an entry is a block number of the sending device or -1 for an unused slot; for each peer the used slots come first, at most 4 of them, a device sends no block to itself, and each device fills all 4 slots of one peer. `face_right`: an entry of at least 2048 names ghost cell (s * 4 + j) * 128 + k only where slot j of the sending peer s is used.
All inputs are finite; a program needn't handle non-finite values.
Results may differ from a plain program's by a relative error of at most 0.0003.
Values sent between devices are 32-bit elements; how exact they have to be, the bound alone decides.
A program may use at most 64 MiB of HBM per device.

v0:
```python
import functools
import jax
import jax.numpy as jnp
from jax import lax
from jax.experimental import pallas as pl
from jax.experimental.pallas import tpu as pltpu
from jax.sharding import PartitionSpec as P

BLK = 128
RIM = 4
GROUP = 13
PIECES = 2

adiabatic = 5.0 / 3.0
courant = 0.3
MESH = pl.DeviceIdType.MESH


def side_state(q, offsets):
    def value(c):
        slopes = q(5 + 3 * c) * offsets[0] + q(6 + 3 * c) * offsets[1] + q(7 + 3 * c) * offsets[2]
        return q(c) + slopes

    return jnp.exp(value(0)), [value(1), value(2), value(3)], jnp.exp(value(4))


def conserved_flux(density, velocity, pressure, normal):
    speed = velocity[0] * normal[0] + velocity[1] * normal[1] + velocity[2] * normal[2]
    square = velocity[0] * velocity[0] + velocity[1] * velocity[1] + velocity[2] * velocity[2]
    energy = pressure / (adiabatic - 1.0) + 0.5 * density * square
    momentum = [density * v for v in velocity]
    conserved = [density] + momentum + [energy]
    flux = (
        [density * speed]
        + [m * speed + pressure * n for m, n in zip(momentum, normal)]
        + [(energy + pressure) * speed]
    )
    return speed, energy, conserved, flux


def star_flux(density, velocity, pressure, normal, speed, energy, conserved, flux, signal, contact, mass_rate):
    factor = mass_rate / (signal - contact)
    jump = contact - speed
    star = (
        [factor]
        + [factor * (v + jump * n) for v, n in zip(velocity, normal)]
        + [factor * (energy / density + jump * (contact + pressure / mass_rate))]
    )
    return [f + signal * (s - u) for f, s, u in zip(flux, star, conserved)]


def hllc(left, right, angles, offsets):
    sin_a = jnp.sin(angles[0])
    normal = [sin_a * jnp.cos(angles[1]), sin_a * jnp.sin(angles[1]), jnp.cos(angles[0])]
    dl, vl, pl_ = side_state(left, offsets[:3])
    dr, vr, pr = side_state(right, offsets[3:])
    ul, el, cl, fl = conserved_flux(dl, vl, pl_, normal)
    ur, er, cr, fr = conserved_flux(dr, vr, pr, normal)
    sound_l = jnp.sqrt(adiabatic * pl_ / dl)
    sound_r = jnp.sqrt(adiabatic * pr / dr)
    signal_l = jnp.minimum(ul - sound_l, ur - sound_r)
    signal_r = jnp.maximum(ul + sound_l, ur + sound_r)
    mass_l = dl * (signal_l - ul)
    mass_r = dr * (signal_r - ur)
    contact = (pr - pl_ + mass_l * ul - mass_r * ur) / (mass_l - mass_r)
    star_l = star_flux(dl, vl, pl_, normal, ul, el, cl, fl, signal_l, contact, mass_l)
    star_r = star_flux(dr, vr, pr, normal, ur, er, cr, fr, signal_r, contact, mass_r)
    out = []
    for a, b, c, d in zip(fl, star_l, star_r, fr):
        inner = jnp.where(contact >= 0, b, jnp.where(signal_r > 0, c, d))
        out.append(jnp.where(signal_l >= 0, a, inner))
    return out


def lane_gather(row, index):
    table = jnp.broadcast_to(row, index.shape)
    return jnp.take_along_axis(table, index, axis=1, mode="promise_in_bounds")


def kernel(dims, send_list, *refs):
    staged = refs[16:29]
    stage_sem = refs[29]
    loads = [pltpu.make_async_copy(source, staged[k], stage_sem.at[k]) for k, source in enumerate(refs[:13])]
    step(dims, send_list, loads, *staged, *refs[13:16], *refs[30:])


def step(
    dims,
    send_list,
    loads,
    prim,
    grad,
    volume,
    face_left,
    face_right,
    face_angles,
    face_area,
    face_offsets,
    rim_left,
    rim_right,
    rim_angles,
    rim_area,
    rim_offsets,
    rate_out,
    new_out,
    step_out,
    outgoing,
    ghosts,
    following,
    table,
    min_own,
    min_sub,
    min_group,
    min_dom,
    gback_send,
    gback_recv,
    rback_send,
    rback_recv,
    cells,
    hi_left,
    lo_left,
    hi_right,
    lo_right,
    angles,
    offsets,
    area,
    gathered_l,
    gathered_r,
    pieces,
    ghost_send_sem,
    ghost_recv_sem,
    rim_send_sem,
    rim_recv_sem,
    min_send_sem,
    min_recv_sem,
    dmin_send_sem,
    dmin_recv_sem,
    gback_send_sem,
    gback_recv_sem,
    rback_send_sem,
    rback_recv_sem,
):
    n_dom, n_sub, capacity, blocks, face_rows = dims
    rows = face_rows + RIM
    group = max(k for k in range(1, GROUP + 1) if rows % k == 0)
    ghost_blocks = n_sub * capacity
    me_dom = lax.axis_index("dom")
    me_sub = lax.axis_index("sub")
    before = lax.rem(me_dom + n_dom - 1, n_dom)
    after = lax.rem(me_dom + 1, n_dom)

    def sub_peer(off):
        return lax.rem(me_sub + off, n_sub)

    def dom_peer(off):
        return lax.rem(me_dom + off, n_dom)

    barrier = pltpu.get_barrier_semaphore()
    for off in range(1, n_sub):
        pl.semaphore_signal(barrier, inc=1, device_id=(me_dom, sub_peer(off)), device_id_type=MESH)
    for off in range(1, n_dom):
        pl.semaphore_signal(barrier, inc=1, device_id=(dom_peer(off), me_sub), device_id_type=MESH)

    for load in loads:
        load.start()
    for k in (0, 1):
        loads[k].wait()

    for h in range(blocks):
        table[h, 0:5, :] = prim[:, h * BLK : (h + 1) * BLK]
        table[h, 5:8, :] = jnp.zeros((3, BLK), jnp.float32)
        table[h, 8:23, :] = grad[:, h * BLK : (h + 1) * BLK]
        table[h, 23:24, :] = jnp.zeros((1, BLK), jnp.float32)

    for off in range(1, n_sub):
        for j in range(capacity):
            block = jnp.maximum(send_list[sub_peer(off) * capacity + j], 0)
            outgoing[off, j] = table[block]

    for k in range(2, len(loads)):
        loads[k].wait()

    for r in range(5):
        for h in range(blocks):
            cells[r, h : h + 1, :] = prim[r : r + 1, h * BLK : (h + 1) * BLK]
    density = jnp.exp(cells[0])
    pressure = jnp.exp(cells[4])
    square = cells[1] * cells[1] + cells[2] * cells[2] + cells[3] * cells[3]
    signal = jnp.sqrt(adiabatic * pressure / density) + jnp.sqrt(square)
    limit = jnp.exp(jnp.log(volume[...]) * (1.0 / 3.0)) / signal
    local_min = jnp.min(limit)
    min_own[...] = jnp.full(min_own.shape, local_min, jnp.float32)

    hi_left[0:face_rows, :] = face_left[...] // BLK
    lo_left[0:face_rows, :] = lax.rem(face_left[...], BLK)
    hi_right[0:face_rows, :] = face_right[...] // BLK
    lo_right[0:face_rows, :] = lax.rem(face_right[...], BLK)
    area[0:face_rows, :] = face_area[...]
    twice = lambda ref: jnp.concatenate([ref[...], ref[...]], 0)
    hi_left[face_rows : face_rows + 8, :] = twice(rim_left) // BLK + (blocks - RIM)
    lo_left[face_rows : face_rows + 8, :] = lax.rem(twice(rim_left), BLK)
    hi_right[face_rows : face_rows + 8, :] = twice(rim_right) // BLK + (blocks + ghost_blocks)
    lo_right[face_rows : face_rows + 8, :] = lax.rem(twice(rim_right), BLK)
    last = me_dom == n_dom - 1
    area[face_rows : face_rows + 8, :] = twice(rim_area)
    for s in range(face_rows):
        for r in range(2):
            angles[r, s : s + 1, :] = face_angles[r : r + 1, s * BLK : (s + 1) * BLK]
        for r in range(6):
            offsets[r, s : s + 1, :] = face_offsets[r : r + 1, s * BLK : (s + 1) * BLK]
    for s in range(8):
        t = s % RIM
        for r in range(2):
            angles[r, face_rows + s : face_rows + s + 1, :] = rim_angles[r : r + 1, t * BLK : (t + 1) * BLK]
        for r in range(6):
            offsets[r, face_rows + s : face_rows + s + 1, :] = rim_offsets[r : r + 1, t * BLK : (t + 1) * BLK]

    tail = pl.ds(face_rows, 8)

    fields = list(range(5)) + list(range(8, 23))

    def gather(hi, lo, entries, names, start):
        match = [hi == name for name in names]
        out = []
        for c, place in enumerate(fields):
            value = start(c)
            for entry, hit in zip(entries, match):
                row = entry[place : place + 1, :]
                value = jnp.where(hit, lane_gather(row, lo), value)
            out.append(value)
        return out

    def gather_into(target, hi, lo, here, entries, names, keep):
        start = (lambda c: target[c, here, :]) if keep else (lambda c: jnp.zeros((8, BLK), jnp.float32))
        for c, value in enumerate(gather(hi[here, :], lo[here, :], entries, names, start)):
            target[c, here, :] = value

    def gather_main(target, hi, lo, entries, names, keep):
        def one(g, carry):
            here = pl.ds(pl.multiple_of(g * 8, 8), 8)
            gather_into(target, hi, lo, here, entries, names, keep)
            return carry

        lax.fori_loop(0, face_rows // 8, one, 0)

    own = [table.at[h] for h in range(blocks)]
    gather_main(gathered_l, hi_left, lo_left, own, range(blocks), False)

    pl.semaphore_wait(barrier, n_sub - 1 + n_dom - 1)

    copies = []

    def ghost_copy(off):
        return pltpu.make_async_remote_copy(
            src_ref=outgoing.at[off],
            dst_ref=ghosts.at[off],
            send_sem=ghost_send_sem.at[off],
            recv_sem=ghost_recv_sem.at[off],
            device_id=(me_dom, sub_peer(off)),
            device_id_type=MESH,
        )

    ghost_copies = [ghost_copy(off) for off in range(1, n_sub)]
    for copy in ghost_copies:
        copy.start()
    rim_copy = pltpu.make_async_remote_copy(
        src_ref=table.at[0:RIM],
        dst_ref=following,
        send_sem=rim_send_sem,
        recv_sem=rim_recv_sem,
        device_id=(before, me_sub),
        device_id_type=MESH,
    )
    rim_copy.start()
    min_copies = [
        pltpu.make_async_remote_copy(
            src_ref=min_own,
            dst_ref=min_sub.at[off],
            send_sem=min_send_sem.at[off],
            recv_sem=min_recv_sem.at[off],
            device_id=(me_dom, sub_peer(off)),
            device_id_type=MESH,
        )
        for off in range(1, n_sub)
    ]
    for copy in min_copies:
        copy.start()

    gather_into(gathered_l, hi_left, lo_left, tail, own[blocks - RIM :], range(blocks - RIM, blocks), False)
    gather_main(gathered_r, hi_right, lo_right, own, range(blocks), False)

    for copy in min_copies:
        copy.wait()
    group_min = min_own[...]
    for off in range(1, n_sub):
        group_min = jnp.minimum(group_min, min_sub[off])
    min_group[...] = group_min

    rim_copy.wait()

    first = blocks + ghost_blocks
    nexts = [following.at[h] for h in range(RIM)]
    gather_into(gathered_r, hi_right, lo_right, tail, nexts, range(first, first + RIM), False)

    dmin_copies = [
        pltpu.make_async_remote_copy(
            src_ref=min_group,
            dst_ref=min_dom.at[off],
            send_sem=dmin_send_sem.at[off],
            recv_sem=dmin_recv_sem.at[off],
            device_id=(dom_peer(off), me_sub),
            device_id_type=MESH,
        )
        for off in range(1, n_dom)
    ]
    for copy in dmin_copies:
        copy.start()

    for copy in ghost_copies:
        copy.wait()

    entries, names = [], []
    for off in range(1, n_sub):
        sender = lax.rem(me_sub + n_sub - off, n_sub)
        for j in range(capacity):
            entries.append(ghosts.at[off, j])
            names.append(blocks + sender * capacity + j)
    gather_main(gathered_r, hi_right, lo_right, entries, names, True)

    def flux_step(g, carry):
        here = pl.ds(pl.multiple_of(g * 8, 8), 8)
        flux = hllc(
            lambda c: gathered_l[c, here, :],
            lambda c: gathered_r[c, here, :],
            [angles[k, here, :] for k in range(2)],
            [offsets[k, here, :] for k in range(6)],
        )
        idle = jnp.logical_and(g * 8 >= face_rows, last)
        for c in range(5):
            value = jnp.where(idle, 0.0, flux[c] * area[here, :])
            big = value.astype(jnp.bfloat16).astype(jnp.float32)
            pieces[c, here, :] = big
            pieces[5 + c, here, :] = value - big
        return carry

    lax.fori_loop(0, (face_rows + 8) // 8, flux_step, 0)

    lane_iota = lax.broadcasted_iota(jnp.int32, (BLK, BLK), 0)

    def one_hot(lo, s):
        return jnp.where(lane_iota == lo[pl.ds(s, 1), :], 1.0, 0.0).astype(jnp.bfloat16)

    def spread(hi, s, first, count, sign):
        place = lax.broadcasted_iota(jnp.int32, (count, BLK), 0) + first
        match = place == hi[pl.ds(s, 1), :]
        parts = []
        for c in range(5 * PIECES):
            value = pieces[c, pl.ds(s, 1), :]
            value = value if sign > 0 else -value
            parts.append(jnp.where(match, value, 0.0))
        return jnp.concatenate(parts, 0).astype(jnp.bfloat16)

    def product(a, b):
        return lax.dot_general(a, b, (((1,), (1,)), ((), ())), preferred_element_type=jnp.float32)

    def fold(total, count):
        total = total.reshape(PIECES, 5, count, BLK)
        return total[0] + total[1]

    away = -(-(ghost_blocks + RIM) // 8) * 8

    def away_step(i, total):
        a = jnp.concatenate([spread(hi_right, i * group + k, blocks, away, -1) for k in range(group)], 1)
        b = jnp.concatenate([one_hot(lo_right, i * group + k) for k in range(group)], 1)
        return total + product(a, b)

    total = lax.fori_loop(0, rows // group, away_step, jnp.zeros((5 * PIECES * away, BLK), jnp.float32))
    total = fold(total, away)
    for s in range(n_sub):
        gback_send[s] = total[:, s * capacity : (s + 1) * capacity, :]
    rback_send[...] = total[:, ghost_blocks : ghost_blocks + RIM, :]
    gback_copies = [
        pltpu.make_async_remote_copy(
            src_ref=gback_send.at[sub_peer(off)],
            dst_ref=gback_recv.at[off],
            send_sem=gback_send_sem.at[off],
            recv_sem=gback_recv_sem.at[off],
            device_id=(me_dom, sub_peer(off)),
            device_id_type=MESH,
        )
        for off in range(1, n_sub)
    ]
    for copy in gback_copies:
        copy.start()
    rback_copy = pltpu.make_async_remote_copy(
        src_ref=rback_send,
        dst_ref=rback_recv,
        send_sem=rback_send_sem,
        recv_sem=rback_recv_sem,
        device_id=(after, me_sub),
        device_id_type=MESH,
    )
    rback_copy.start()

    def local_step(i, total):
        a = [spread(hi_left, i * group + k, 0, blocks, 1) for k in range(group)]
        a += [spread(hi_right, i * group + k, 0, blocks, -1) for k in range(group)]
        b = [one_hot(lo_left, i * group + k) for k in range(group)]
        b += [one_hot(lo_right, i * group + k) for k in range(group)]
        return total + product(jnp.concatenate(a, 1), jnp.concatenate(b, 1))

    total = lax.fori_loop(0, rows // group, local_step, jnp.zeros((5 * PIECES * blocks, BLK), jnp.float32))
    net = fold(total, blocks)

    for copy in dmin_copies:
        copy.wait()
    smallest = min_group[...]
    for off in range(1, n_dom):
        smallest = jnp.minimum(smallest, min_dom[off])
    time_step = courant * smallest
    step_out[0] = jnp.min(time_step)
    time_step = time_step[0:1, :]

    rback_copy.wait()
    for copy in gback_copies:
        copy.wait()

    place = lax.broadcasted_iota(jnp.int32, (blocks, BLK), 0)
    density = jnp.exp(cells[0])
    pressure = jnp.exp(cells[4])
    square = cells[1] * cells[1] + cells[2] * cells[2] + cells[3] * cells[3]
    energy = pressure / (adiabatic - 1.0) + 0.5 * density * square
    conserved = [density, density * cells[1], density * cells[2], density * cells[3], energy]
    for c in range(5):
        sums = net[c]
        for h in range(RIM):
            sums = sums + jnp.where(place == h, rback_recv[c, h : h + 1, :], 0.0)
        for off in range(1, n_sub):
            sender = lax.rem(me_sub + n_sub - off, n_sub)
            for j in range(capacity):
                wanted = send_list[sender * capacity + j]
                sums = sums + jnp.where(place == wanted, gback_recv[off, c, j : j + 1, :], 0.0)
        rate = -sums / volume[...]
        rate_out[c] = rate
        new_out[c] = conserved[c] + time_step * rate


def body(mesh_sizes, *args):
    (primitive, gradient, volume, face_left, face_right, face_angles, face_area, face_offsets) = args[:8]
    (rim_left, rim_right, rim_angles, rim_area, rim_offsets, send_list) = args[8:]
    n_dom, n_sub = mesh_sizes
    cells = primitive.shape[1]
    blocks = cells // BLK
    face_rows = face_left.shape[0] // BLK
    capacity = send_list.shape[0] // n_sub
    padded = face_rows + 8
    dims = (n_dom, n_sub, capacity, blocks, face_rows)
    f32, i32 = jnp.float32, jnp.int32
    vmem = pl.BlockSpec(memory_space=pltpu.VMEM)
    smem = pl.BlockSpec(memory_space=pltpu.SMEM)
    sem = pltpu.SemaphoreType.DMA
    operands = (
        primitive,
        gradient,
        volume.reshape(blocks, BLK),
        face_left.reshape(face_rows, BLK),
        face_right.reshape(face_rows, BLK),
        face_angles,
        face_area.reshape(face_rows, BLK),
        face_offsets,
        rim_left.reshape(RIM, BLK),
        rim_right.reshape(RIM, BLK),
        rim_angles,
        rim_area.reshape(RIM, BLK),
        rim_offsets,
    )
    rate, new, step = pl.pallas_call(
        functools.partial(kernel, dims),
        out_shape=(
            jax.ShapeDtypeStruct((5, blocks, BLK), f32),
            jax.ShapeDtypeStruct((5, blocks, BLK), f32),
            jax.ShapeDtypeStruct((1,), f32),
        ),
        in_specs=[smem] + [pl.BlockSpec(memory_space=pl.ANY)] * 13,
        out_specs=(vmem, vmem, smem),
        scratch_shapes=[pltpu.VMEM(x.shape, x.dtype) for x in operands]
        + [
            sem((len(operands),)),
            pltpu.VMEM((n_sub, capacity, 24, BLK), f32),
            pltpu.VMEM((n_sub, capacity, 24, BLK), f32),
            pltpu.VMEM((RIM, 24, BLK), f32),
            pltpu.VMEM((blocks, 24, BLK), f32),
            pltpu.VMEM((8, BLK), f32),
            pltpu.VMEM((n_sub, 8, BLK), f32),
            pltpu.VMEM((8, BLK), f32),
            pltpu.VMEM((n_dom, 8, BLK), f32),
            pltpu.VMEM((n_sub, 5, capacity, BLK), f32),
            pltpu.VMEM((n_sub, 5, capacity, BLK), f32),
            pltpu.VMEM((5, RIM, BLK), f32),
            pltpu.VMEM((5, RIM, BLK), f32),
            pltpu.VMEM((5, blocks, BLK), f32),
            pltpu.VMEM((padded, BLK), i32),
            pltpu.VMEM((padded, BLK), i32),
            pltpu.VMEM((padded, BLK), i32),
            pltpu.VMEM((padded, BLK), i32),
            pltpu.VMEM((2, padded, BLK), f32),
            pltpu.VMEM((6, padded, BLK), f32),
            pltpu.VMEM((padded, BLK), f32),
            pltpu.VMEM((20, padded, BLK), f32),
            pltpu.VMEM((20, padded, BLK), f32),
            pltpu.VMEM((5 * PIECES, padded, BLK), f32),
            sem((n_sub,)),
            sem((n_sub,)),
            sem,
            sem,
            sem((n_sub,)),
            sem((n_sub,)),
            sem((n_dom,)),
            sem((n_dom,)),
            sem((n_sub,)),
            sem((n_sub,)),
            sem,
            sem,
        ],
        compiler_params=pltpu.CompilerParams(collective_id=0, has_side_effects=True),
        name="hydro_step",
    )(
        send_list,
        *operands,
    )
    return rate.reshape(5, cells), new.reshape(5, cells), step.reshape(())


def solution(mesh):
    both = ("dom", "sub")
    wide, flat = P(None, both), P(both)
    in_specs = (wide, wide, flat, flat, flat, wide, flat, wide, flat, flat, wide, flat, wide, flat)
    out_specs = (wide, wide, P())
    step = functools.partial(body, (mesh.shape["dom"], mesh.shape["sub"]))
    return jax.shard_map(step, mesh=mesh, in_specs=in_specs, out_specs=out_specs, check_vma=False)
```

profile of v0, /device:TPU:0, one launch (start us, length us, event | category | flops | bytes accessed | tf_op | source)
XLA Modules:
  0.0 26.2 jit_solution(5494996939188719743)
XLA Ops:
  0.6 22.4 %hydro_step.1 = (f32[5,16,128]{2,1,0:T(8,128)}, f32[5,16,128]{2,1,0:T(8,128)}, f32[1]{0:T(128)}) custom-call(s32[16]{0:T(128)} %send_list.1, f32[5,2048]{1,0:T(8,128)} %refs_0_.1, f32[15,2048]{1,0:T(8,128)} %refs_1_.1, f32[16,128]{1,0:T(8,128)} %bitcast.19, s32[48,128]{1,0:T(8,128)} %bitcast.16, s32[48,128]{1,0:T(8,128)} %bitcast.17, f32[2,6144]{1,0:T(2,128)} %refs_5_.1, ...), custom_call_target="tpu_custom_call" | custom-call | tf_op jit(solution)/shard_map/hydro_step/pallas_call | solution.py:477
  23.0 1.5 %copy_bitcast_fusion = (f32[5,2048]{1,0:T(8,128)}, f32[5,2048]{1,0:T(8,128)}) fusion(f32[1,5,16,128]{3,2,1,0:T(8,128)} %bitcast.15, f32[1,5,16,128]{3,2,1,0:T(8,128)} %bitcast.14), kind=kLoop, calls=%fused_computation | loop fusion | bytes 163840 | tf_op jit(solution)/shard_map/reshape | solution.py:531
where the time goes:
time: 26.4 us; the launch traced here: 26.2 us
  Pallas kernels  22.4 us (85%)
  between operations  2.33 us (9%)
  local copies, waits for them, and re-layouts  1.48 us (6%)
    pallas_call x1, Pallas kernels, body(): pl.pallas_call(functools.partial(kernel, dims), out_shape=(jax.ShapeDtype...  22.4 us
    reshape x1, local copies, waits for them, and re-layouts, body(): return (rate.reshape(5, cells), new.reshape(5, cells), step.reshape(()))  1.48 us

commit v1 on v0

v1 whole, which is shorter than its diff:
```python
import functools
import jax
import jax.numpy as jnp
from jax import lax
from jax.experimental import pallas as pl
from jax.experimental.pallas import tpu as pltpu
from jax.sharding import PartitionSpec as P

BLK = 128
RIM = 4
GROUP = 13
PIECES = 2
RAW = 6
PACKED = 7
GRAD_MAX = 1.5
GRAD_STEPS = 32767.0

adiabatic = 5.0 / 3.0
courant = 0.3
MESH = pl.DeviceIdType.MESH


def sin_cos(x):
    turns = jnp.floor(x * 0.63661977236 + 0.5)
    r = (x - turns * 1.57079637050628662109375) - turns * -4.37113900018624283e-8
    r2 = r * r
    sine = r + r * r2 * (-1.6666667163e-1 + r2 * (8.3333337680e-3 + r2 * (-1.9841270114e-4 + r2 * 2.7557314297e-6)))
    cosine = 1.0 + r2 * (-0.5 + r2 * (4.1666667908e-2 + r2 * (-1.3888889225e-3 + r2 * 2.4801587642e-5)))
    odd = jnp.abs(turns) == 1.0
    s = jnp.where(odd, cosine, sine)
    c = jnp.where(odd, sine, cosine)
    s = jnp.where((turns < 0.0) | (turns > 1.0), -s, s)
    c = jnp.where((turns > 0.0) | (turns < -1.0), -c, c)
    return s, c


def pack_pair(a, b):
    scale = GRAD_STEPS / GRAD_MAX
    high = (a * scale + 32768.5).astype(jnp.int32)
    low = (b * scale + 32768.5).astype(jnp.int32)
    return lax.shift_left(high, jnp.full_like(high, 16)) + (low + jnp.int32(-(2**31)))


def gradients(raw, packed):
    out = [None] * 15
    for w in range(PACKED):
        word = packed(w)
        out[w] = lax.shift_right_arithmetic(word, jnp.full_like(word, 16)).astype(jnp.float32)
        out[w + 8] = ((word & 65535) - 32768).astype(jnp.float32)
    out[7] = raw(5) * (GRAD_STEPS / GRAD_MAX)
    return out


def side_state(raw, packed, offsets):
    step = GRAD_MAX / GRAD_STEPS
    offsets = [r * step for r in offsets]
    slope = gradients(raw, packed)
    values = [
        raw(c) + (slope[3 * c] * offsets[0] + slope[3 * c + 1] * offsets[1] + slope[3 * c + 2] * offsets[2])
        for c in range(5)
    ]
    sound = jnp.exp((values[4] - values[0]) * 0.5) * (adiabatic**0.5)
    return jnp.exp(values[0]), values[1:4], jnp.exp(values[4]), sound


def dot3(a, b):
    return a[0] * b[0] + a[1] * b[1] + a[2] * b[2]


def hllc(normal, left, right):
    dl, vl, pl_, cl, ul = left
    dr, vr, pr, cr = right
    ur = dot3(vr, normal)
    signal_l = jnp.minimum(ul - cl, ur - cr)
    signal_r = jnp.maximum(ul + cl, ur + cr)
    mass_l = dl * (signal_l - ul)
    mass_r = dr * (signal_r - ur)
    contact = (pr - pl_ + mass_l * ul - mass_r * ur) / (mass_l - mass_r)
    outer = signal_l >= 0
    from_left = jnp.logical_or(outer, contact >= 0)
    starred = jnp.where(from_left, signal_l, -signal_r) < 0
    pick = lambda a, b: jnp.where(from_left, a, b)
    density, pressure, speed, sound = pick(dl, dr), pick(pl_, pr), pick(ul, ur), pick(cl, cr)
    velocity = [pick(a, b) for a, b in zip(vl, vr)]
    signal, mass_rate = pick(signal_l, signal_r), pick(mass_l, mass_r)
    specific = sound * sound * (1.0 / (adiabatic * (adiabatic - 1.0))) + 0.5 * dot3(velocity, velocity)
    energy = density * specific
    jump = contact - speed
    factor = mass_rate / (signal - contact)
    rise = jnp.where(starred, signal * (factor - density), 0.0)
    push = jnp.where(starred, signal * factor * jump, 0.0)
    rate = density * speed
    out = [rate + rise]
    along = pressure + push
    carry = rate + rise
    for v, n in zip(velocity, normal):
        out.append(carry * v + along * n)
    out.append((energy + pressure) * speed + rise * specific + push * (contact + pressure / mass_rate))
    return out


def lane_gather(row, index):
    table = jnp.broadcast_to(row, index.shape)
    return jnp.take_along_axis(table, index, axis=1, mode="promise_in_bounds")


def flip(index, mask, size):
    out, bit = index, 1
    while bit < size:
        if mask & bit:
            out = out + bit * (1 - 2 * lax.rem(lax.div(index, bit), 2))
        bit *= 2
    return out


def kernel(
    dims,
    send_hbm,
    prim_rows,
    grad_hbm,
    volume_hbm,
    left_hbm,
    right_hbm,
    angles_hbm,
    area_hbm,
    offsets_hbm,
    rim_left_hbm,
    rim_right_hbm,
    rim_angles_hbm,
    rim_area_hbm,
    rim_offsets_hbm,
    rate_out,
    new_out,
    step_out,
    send_list,
    prim,
    cells,
    grad,
    volume,
    face_left,
    face_right,
    angles,
    area,
    offsets,
    rim_left,
    rim_right,
    outgoing,
    ghosts,
    next_prim,
    next_grad,
    own_packed,
    ghost_packed,
    next_packed,
    min_own,
    mins,
    min_spare,
    min_base,
    prefix_send,
    prefix_recv,
    gback_send,
    gback_recv,
    rback_send,
    rback_recv,
    hi_left,
    lo_left,
    hi_right,
    lo_right,
    left_raw,
    left_packed,
    right_raw,
    right_packed,
    ready,
    pieces,
    load_sem,
    ghost_send_sem,
    ghost_recv_sem,
    rim_send_sem,
    rim_recv_sem,
    min_send_sem,
    min_recv_sem,
    prefix_send_sem,
    prefix_recv_sem,
    gback_send_sem,
    gback_recv_sem,
    rback_send_sem,
    rback_recv_sem,
    hello_above,
    hello_next,
):
    n_dom, n_sub, capacity, blocks, face_rows = dims
    rows = face_rows + RIM
    group = max(k for k in range(1, GROUP + 1) if rows % k == 0)
    ghost_blocks = n_sub * capacity
    me_dom = lax.axis_index("dom")
    me_sub = lax.axis_index("sub")
    plane = 2 if n_dom % 2 == 0 else 1
    planes = n_dom // plane
    my_plane = lax.div(me_dom, plane)
    base_dom = my_plane * plane
    last = me_dom == n_dom - 1
    first = me_dom == 0
    power = n_sub & (n_sub - 1) == 0

    def to_peer(k):
        return flip(me_sub, k, n_sub) if power else lax.rem(me_sub + k, n_sub)

    def from_peer(k):
        return flip(me_sub, k, n_sub) if power else lax.rem(me_sub + n_sub - k, n_sub)

    far_first = list(range(n_sub - 1, 0, -1))

    tail = pl.ds(face_rows, RIM)
    pairs = [(send_hbm, send_list), (prim_rows, prim)]
    pairs += [(grad_hbm.at[:, h * BLK : (h + 1) * BLK], grad.at[h]) for h in range(blocks)]
    early = len(pairs)
    pairs += [(prim_rows.at[:, r, :], cells.at[r]) for r in range(5)]
    pairs += [(volume_hbm, volume)]
    middle = len(pairs)
    pairs += [(left_hbm, face_left), (right_hbm, face_right), (rim_left_hbm, rim_left), (rim_right_hbm, rim_right)]
    indices = len(pairs)
    pairs += [(angles_hbm.at[:, r, :], angles.at[r, 0:face_rows, :]) for r in range(2)]
    pairs += [(offsets_hbm.at[:, r, :], offsets.at[r, 0:face_rows, :]) for r in range(6)]
    pairs += [(area_hbm, area.at[0:face_rows, :])]
    pairs += [(rim_angles_hbm.at[:, r, :], angles.at[r, tail, :]) for r in range(2)]
    pairs += [(rim_offsets_hbm.at[:, r, :], offsets.at[r, tail, :]) for r in range(6)]
    pairs += [(rim_area_hbm, area.at[tail, :])]
    loads = [pltpu.make_async_copy(a, b, load_sem.at[k]) for k, (a, b) in enumerate(pairs)]
    for load in loads[:middle]:
        load.start()

    barrier = pltpu.get_barrier_semaphore()
    for step in range(plane):
        dom = base_dom + lax.rem(me_dom + step, plane)
        for k in range(n_sub):
            if step or k:
                pl.semaphore_signal(barrier, inc=1, device_id=(dom, to_peer(k)), device_id_type=MESH)

    def greet(p, carry):
        for step in range(plane):
            for k in range(n_sub):
                pl.semaphore_signal(barrier, inc=1, device_id=(p * plane + step, k), device_id_type=MESH)
        return carry

    for load in loads[middle:]:
        load.start()
    lax.fori_loop(my_plane + 1, planes, greet, 0)

    for load in loads[:early]:
        load.wait()
    for k in far_first:
        for j in range(capacity):
            block = jnp.maximum(send_list[to_peer(k) * capacity + j], 0)
            slopes, centres = grad[block], prim[block]
            outgoing[k, 8 * j : 8 * j + 8, :] = slopes[0:8]
            low = 8 * capacity + 8 * j
            outgoing[k, low : low + 7, :] = slopes[8:15]
            outgoing[k, low + 7 : low + 8, :] = centres[0:1]
            outgoing[k, 16 * capacity + 4 * j : 16 * capacity + 4 * j + 4, :] = centres[1:5]

    for load in loads[early:middle]:
        load.wait()
    signal = jnp.exp((cells[4] - cells[0]) * 0.5) * (adiabatic**0.5) + jnp.sqrt(
        cells[1] * cells[1] + cells[2] * cells[2] + cells[3] * cells[3]
    )
    limit = jnp.exp(jnp.log(volume[...]) * (1.0 / 3.0)) / signal
    min_own[...] = jnp.min(limit, axis=0, keepdims=True)

    for h in range(blocks):
        own_packed[h, 0:PACKED, :] = pack_pair(grad[h, 0:7, :], grad[h, 8:15, :])

    for load in loads[middle:indices]:
        load.wait()
    twice = lambda ref: jnp.concatenate([ref[...], ref[...]], 0)
    main = slice(0, face_rows)
    over = slice(face_rows, face_rows + 8)
    high = lambda x: lax.shift_right_logical(x, jnp.full_like(x, 7))
    hi_left[main, :] = high(face_left[...])
    lo_left[main, :] = face_left[...] & (BLK - 1)
    hi_right[main, :] = high(face_right[...])
    lo_right[main, :] = face_right[...] & (BLK - 1)
    hi_left[over, :] = high(twice(rim_left)) + (blocks - RIM)
    lo_left[over, :] = twice(rim_left) & (BLK - 1)
    hi_right[over, :] = high(twice(rim_right)) + (blocks + ghost_blocks)
    lo_right[over, :] = twice(rim_right) & (BLK - 1)

    count = plane * n_sub - 1 + plane * n_sub * my_plane
    pl.semaphore_wait(barrier, count)

    def remote(src, dst, send, recv, dom, sub):
        return pltpu.make_async_remote_copy(
            src_ref=src, dst_ref=dst, send_sem=send, recv_sem=recv, device_id=(dom, sub), device_id_type=MESH
        )

    def min_copy(dom, sub, p):
        return remote(min_own, mins.at[me_dom, me_sub], min_send_sem.at[p], min_recv_sem.at[my_plane], dom, sub)

    for step in range(plane):
        dom = base_dom + lax.rem(me_dom + step, plane)
        for k in range(n_sub):
            if step or k:
                min_copy(dom, to_peer(k), my_plane).start()

    ghost_copies = {
        k: remote(outgoing.at[k], ghosts.at[k], ghost_send_sem.at[k], ghost_recv_sem.at[k], me_dom, to_peer(k))
        for k in far_first
    }
    for k in far_first:
        ghost_copies[k].start()
    rim_copies = [
        remote(src.at[0:RIM], dst, rim_send_sem.at[i], rim_recv_sem.at[i], me_dom - 1, me_sub)
        for i, (src, dst) in enumerate([(prim, next_prim), (grad, next_grad)])
    ]

    def tell(p, carry):
        for step in range(plane):
            for k in range(n_sub):
                min_copy(p * plane + step, k, p).start()
        return carry

    @pl.when(jnp.logical_not(first))
    def _():
        for copy in rim_copies:
            copy.start()

    lax.fori_loop(0, my_plane, tell, 0)

    @pl.when(my_plane > 0)
    def _():
        pl.semaphore_signal(hello_above, inc=1, device_id=(me_dom - plane, me_sub), device_id_type=MESH)

    @pl.when(jnp.logical_and(lax.rem(me_dom, plane) == 0, me_dom > 0))
    def _():
        pl.semaphore_signal(hello_next, inc=1, device_id=(me_dom - 1, me_sub), device_id_type=MESH)

    def own_row(h):
        def row(c):
            if c < 5:
                return cells[c, h : h + 1, :]
            if c == 5:
                return grad[h, 7:8, :]
            return own_packed[h, c - RAW : c - RAW + 1, :]

        return row

    def ghost_row(k, j):
        def row(c):
            if c == 0:
                at = 8 * capacity + 8 * j + 7
            elif c < 5:
                at = 16 * capacity + 4 * j + c - 1
            elif c == 5:
                at = 8 * j + 7
            else:
                return ghost_packed[k, j, c - RAW : c - RAW + 1, :]
            return ghosts[k, at : at + 1, :]

        return row

    def next_row(h):
        def row(c):
            if c < 5:
                return next_prim[h, c : c + 1, :]
            if c == 5:
                return next_grad[h, 7:8, :]
            return next_packed[h, c - RAW : c - RAW + 1, :]

        return row

    def gather_into(raw, packed, hi, lo, starts, sources, names, keep):
        at = [pl.ds(s, 8) for s in starts]
        index = [lo[here, :] for here in at]
        wanted = [hi[here, :] for here in at]
        match = [[w == name for name in names] for w in wanted]
        for c in range(RAW + PACKED):
            target, place = (raw, c) if c < RAW else (packed, c - RAW)
            values = [target[place, here, :] for here in at] if keep else [None] * len(at)
            for n, row in enumerate(sources):
                line = row(c)
                for i in range(len(at)):
                    got = lane_gather(line, index[i])
                    values[i] = got if values[i] is None else jnp.where(match[i][n], got, values[i])
            for here, value in zip(at, values):
                target[place, here, :] = value

    def gather_main(raw, packed, hi, lo, sources, names, keep, width):
        while (face_rows // 8) % width:
            width -= 1

        def one(g, carry):
            starts = [pl.multiple_of(g * (8 * width) + 8 * i, 8) for i in range(width)]
            gather_into(raw, packed, hi, lo, starts, sources, names, keep)
            return carry

        lax.fori_loop(0, face_rows // (8 * width), one, 0)

    own = [own_row(h) for h in range(blocks)]
    gather_main(left_raw, left_packed, hi_left, lo_left, own, range(blocks), False, 2)
    gather_into(
        left_raw, left_packed, hi_left, lo_left, [face_rows], own[blocks - RIM :], range(blocks - RIM, blocks), False
    )
    gather_main(right_raw, right_packed, hi_right, lo_right, own, range(blocks), False, 2)

    for load in loads[indices:]:
        load.wait()
    for r in range(2):
        angles[r, face_rows + RIM : face_rows + 8, :] = angles[r, tail, :]
    for r in range(6):
        offsets[r, face_rows + RIM : face_rows + 8, :] = offsets[r, tail, :]
    area[face_rows + RIM : face_rows + 8, :] = area[tail, :]

    def left_step(g, carry):
        here = pl.ds(pl.multiple_of(g * 8, 8), 8)
        sin_a, cos_a = sin_cos(angles[0, here, :])
        sin_b, cos_b = sin_cos(angles[1, here, :])
        normal = [sin_a * cos_b, sin_a * sin_b, cos_a]
        density, velocity, pressure, sound = side_state(
            lambda c: left_raw[c, here, :],
            lambda w: left_packed[w, here, :],
            [offsets[k, here, :] for k in range(3)],
        )
        values = normal + [density] + velocity + [pressure, sound, dot3(velocity, normal)]
        for k, value in enumerate(values):
            ready[k, here, :] = value
        return carry

    lax.fori_loop(0, (face_rows + 8) // 8, left_step, 0)

    def await_mins(semaphore, count):
        some = min_spare.at[0:count]
        pltpu.make_async_copy(some, some, semaphore).wait()

    def own_plane_min():
        await_mins(min_recv_sem.at[my_plane], plane * n_sub - 1)
        small = min_own[...]
        for step in range(1, plane * n_sub):
            dom = base_dom + lax.rem(me_dom + step // n_sub, plane)
            sub = lax.rem(me_sub + step, n_sub)
            small = jnp.minimum(small, mins[dom, sub])
        min_base[...] = small

        @pl.when(my_plane > 0)
        def _():
            prefix_copy.wait_recv()
            min_base[...] = jnp.minimum(min_base[...], prefix_recv[...])

    prefix_copy = remote(prefix_send, prefix_recv, prefix_send_sem, prefix_recv_sem, me_dom + plane, me_sub)

    def pass_on(mine):
        @pl.when(mine)
        def _():
            own_plane_min()
            prefix_send[...] = min_base[...]
            pl.semaphore_wait(hello_above, 1)
            prefix_copy.start()

    not_top = my_plane < planes - 1
    pass_on(jnp.logical_and(not_top, my_plane == 0))

    def pack_ghosts(k):
        for j in range(capacity):
            low = 8 * capacity + 8 * j
            ghost_packed[k, j, 0:PACKED, :] = pack_pair(ghosts[k, 8 * j : 8 * j + 7, :], ghosts[k, low : low + 7, :])

    def ghost_pass(ks):
        for k in ks:
            ghost_copies[k].wait()
            pack_ghosts(k)
        sources = [ghost_row(k, j) for k in ks for j in range(capacity)]
        names = [blocks + from_peer(k) * capacity + j for k in ks for j in range(capacity)]
        gather_main(right_raw, right_packed, hi_right, lo_right, sources, names, True, 3)

    ghost_pass([1])

    @pl.when(last)
    def _():
        next_prim[...] = jnp.zeros_like(next_prim)
        next_grad[...] = jnp.zeros_like(next_grad)

    @pl.when(jnp.logical_not(last))
    def _():
        for copy in rim_copies:
            copy.wait_recv()

    for h in range(RIM):
        next_packed[h, 0:PACKED, :] = pack_pair(next_grad[h, 0:7, :], next_grad[h, 8:15, :])
    start = blocks + ghost_blocks
    gather_into(
        right_raw,
        right_packed,
        hi_right,
        lo_right,
        [face_rows],
        [next_row(h) for h in range(RIM)],
        range(start, start + RIM),
        False,
    )

    ghost_pass([k for k in far_first if k > 1])
    pass_on(jnp.logical_and(not_top, lax.rem(my_plane, 2) == 1))

    def flux_step(g, carry):
        here = pl.ds(pl.multiple_of(g * 8, 8), 8)
        kept = [ready[k, here, :] for k in range(10)]
        right = side_state(
            lambda c: right_raw[c, here, :],
            lambda w: right_packed[w, here, :],
            [offsets[k, here, :] for k in range(3, 6)],
        )
        flux = hllc(kept[:3], (kept[3], kept[4:7], kept[7], kept[8], kept[9]), right)
        idle = jnp.logical_and(g * 8 >= face_rows, last)
        for c in range(5):
            value = jnp.where(idle, 0.0, flux[c] * area[here, :])
            big = value.astype(jnp.bfloat16).astype(jnp.float32)
            pieces[c, here, :] = big
            pieces[5 + c, here, :] = value - big
        return carry

    lax.fori_loop(0, (face_rows + 8) // 8, flux_step, 0)
    pass_on(functools.reduce(jnp.logical_and, [not_top, lax.rem(my_plane, 2) == 0, my_plane > 0]))

    lane_iota = lax.broadcasted_iota(jnp.int32, (BLK, BLK), 0)

    def one_hot(lo, s):
        return jnp.where(lane_iota == lo[pl.ds(s, 1), :], 1.0, 0.0).astype(jnp.bfloat16)

    def spread(hi, s, place, sign):
        match = place == hi[pl.ds(s, 1), :]
        parts = []
        for c in range(5 * PIECES):
            value = pieces[c, pl.ds(s, 1), :]
            value = value if sign > 0 else -value
            parts.append(jnp.where(match, value, 0.0))
        return jnp.concatenate(parts, 0).astype(jnp.bfloat16)

    def product(a, b):
        return lax.dot_general(a, b, (((1,), (1,)), ((), ())), preferred_element_type=jnp.float32)

    def fold(total, count):
        total = total.reshape(PIECES, 5, count, BLK)
        return total[0] + total[1]

    sent = (n_sub - 1) * capacity
    away = -(-(sent + RIM) // 8) * 8
    spot = lax.broadcasted_iota(jnp.int32, (away, BLK), 0)
    away_place = spot - sent + (blocks + ghost_blocks)
    for k in range(1, n_sub):
        lower = (k - 1) * capacity
        away_place = jnp.where(
            (spot >= lower) & (spot < lower + capacity), spot - lower + (blocks + from_peer(k) * capacity), away_place
        )
    own_place = lax.broadcasted_iota(jnp.int32, (blocks, BLK), 0)

    def away_step(i, total):
        a = jnp.concatenate([spread(hi_right, i * group + k, away_place, -1) for k in range(group)], 1)
        b = jnp.concatenate([one_hot(lo_right, i * group + k) for k in range(group)], 1)
        return total + product(a, b)

    total = lax.fori_loop(0, rows // group, away_step, jnp.zeros((5 * PIECES * away, BLK), jnp.float32))
    total = fold(total, away)
    for k in range(1, n_sub):
        gback_send[k] = total[:, (k - 1) * capacity : k * capacity, :]
    rback_send[...] = total[:, sent : sent + RIM, :]
    gback_copies = {
        k: remote(
            gback_send.at[k], gback_recv.at[k], gback_send_sem.at[k], gback_recv_sem.at[k], me_dom, from_peer(k)
        )
        for k in far_first
    }
    for k in far_first:
        gback_copies[k].start()
    rback_copy = remote(rback_send, rback_recv, rback_send_sem, rback_recv_sem, me_dom + 1, me_sub)

    @pl.when(jnp.logical_and(lax.rem(me_dom, plane) == plane - 1, jnp.logical_not(last)))
    def _():
        pl.semaphore_wait(hello_next, 1)

    @pl.when(jnp.logical_not(last))
    def _():
        rback_copy.start()

    def local_step(i, total):
        a = [spread(hi_left, i * group + k, own_place, 1) for k in range(group)]
        a += [spread(hi_right, i * group + k, own_place, -1) for k in range(group)]
        b = [one_hot(lo_left, i * group + k) for k in range(group)]
        b += [one_hot(lo_right, i * group + k) for k in range(group)]
        return total + product(jnp.concatenate(a, 1), jnp.concatenate(b, 1))

    total = lax.fori_loop(0, rows // group, local_step, jnp.zeros((5 * PIECES * blocks, BLK), jnp.float32))
    net = fold(total, blocks)

    @pl.when(jnp.logical_not(not_top))
    def _():
        own_plane_min()

    def later(p, small):
        await_mins(min_recv_sem.at[p], plane * n_sub)
        for step in range(plane):
            for k in range(n_sub):
                small = jnp.minimum(small, mins[p * plane + step, k])
        return small

    smallest = lax.fori_loop(my_plane + 1, planes, later, min_base[...])
    time_step = courant * jnp.min(smallest, axis=1, keepdims=True)
    step_out[0] = courant * jnp.min(smallest)

    @pl.when(first)
    def _():
        rback_recv[...] = jnp.zeros_like(rback_recv)

    @pl.when(jnp.logical_not(first))
    def _():
        rback_copy.wait_recv()

    for k in far_first:
        gback_copies[k].wait()

    square = cells[1] * cells[1] + cells[2] * cells[2] + cells[3] * cells[3]
    density = jnp.exp(cells[0])
    energy = jnp.exp(cells[4]) / (adiabatic - 1.0) + 0.5 * density * square
    conserved = [density, density * cells[1], density * cells[2], density * cells[3], energy]
    inverse = -1.0 / volume[...]
    for c in range(5):
        sums = net[c]
        for h in range(RIM):
            sums = sums + jnp.where(own_place == h, rback_recv[c, h : h + 1, :], 0.0)
        for k in range(1, n_sub):
            for j in range(capacity):
                wanted = send_list[to_peer(k) * capacity + j]
                sums = sums + jnp.where(own_place == wanted, gback_recv[k, c, j : j + 1, :], 0.0)
        rate = sums * inverse
        new = conserved[c] + time_step * rate
        rate_out[:, c, :] = rate
        new_out[:, c, :] = new

    @pl.when(jnp.logical_not(first))
    def _():
        for copy in rim_copies:
            copy.wait_send()

    @pl.when(jnp.logical_not(last))
    def _():
        rback_copy.wait_send()

    @pl.when(not_top)
    def _():
        prefix_copy.wait_send()

    await_mins(min_send_sem.at[my_plane], plane * n_sub - 1)

    def told(p, carry):
        await_mins(min_send_sem.at[p], plane * n_sub)
        return carry

    lax.fori_loop(0, my_plane, told, 0)


def finish(rate, new, step, rate_out, new_out, step_out, sems):
    pairs = ((rate, rate_out), (new, new_out), (step, step_out))
    copies = [pltpu.make_async_copy(a, b, sems.at[k]) for k, (a, b) in enumerate(pairs)]
    for copy in copies:
        copy.start()
    for copy in copies:
        copy.wait()


def by_block(x):
    return x.reshape(x.shape[0], x.shape[1] // BLK, BLK).transpose(1, 0, 2)


def body(mesh_sizes, *args):
    (primitive, gradient, volume, face_left, face_right, face_angles, face_area, face_offsets) = args[:8]
    (rim_left, rim_right, rim_angles, rim_area, rim_offsets, send_list) = args[8:]
    n_dom, n_sub = mesh_sizes
    cells = primitive.shape[1]
    blocks = cells // BLK
    face_rows = face_left.shape[0] // BLK
    capacity = send_list.shape[0] // n_sub
    padded = face_rows + 8
    dims = (n_dom, n_sub, capacity, blocks, face_rows)
    f32, i32 = jnp.float32, jnp.int32
    planes = n_dom // (2 if n_dom % 2 == 0 else 1)
    away = -(-((n_sub - 1) * capacity + RIM) // 8) * 8
    sem = pltpu.SemaphoreType.DMA
    operands = (
        send_list,
        by_block(primitive),
        gradient,
        volume.reshape(blocks, BLK),
        face_left.reshape(face_rows, BLK),
        face_right.reshape(face_rows, BLK),
        by_block(face_angles),
        face_area.reshape(face_rows, BLK),
        by_block(face_offsets),
        rim_left.reshape(RIM, BLK),
        rim_right.reshape(RIM, BLK),
        by_block(rim_angles),
        rim_area.reshape(RIM, BLK),
        by_block(rim_offsets),
    )
    vmem = pltpu.VMEM
    rate, new, step = pl.pallas_call(
        functools.partial(kernel, dims),
        out_shape=(
            vmem((blocks, 5, BLK), f32),
            vmem((blocks, 5, BLK), f32),
            pltpu.SMEM((1,), f32),
        ),
        in_specs=[pl.BlockSpec(memory_space=pl.ANY)] * len(operands),
        out_specs=(pl.BlockSpec(memory_space=pltpu.VMEM), pl.BlockSpec(memory_space=pltpu.VMEM), pl.BlockSpec(memory_space=pltpu.SMEM)),
        scratch_shapes=[
            pltpu.SMEM(send_list.shape, i32),
            vmem((blocks, 5, BLK), f32),
            vmem((5, blocks, BLK), f32),
            vmem((blocks, 15, BLK), f32),
            vmem((blocks, BLK), f32),
            vmem((face_rows, BLK), i32),
            vmem((face_rows, BLK), i32),
            vmem((2, padded, BLK), f32),
            vmem((padded, BLK), f32),
            vmem((6, padded, BLK), f32),
            vmem((RIM, BLK), i32),
            vmem((RIM, BLK), i32),
            vmem((n_sub, 20 * capacity, BLK), f32),
            vmem((n_sub, 20 * capacity, BLK), f32),
            vmem((RIM, 5, BLK), f32),
            vmem((RIM, 15, BLK), f32),
            vmem((blocks, 8, BLK), i32),
            vmem((n_sub, capacity, 8, BLK), i32),
            vmem((RIM, 8, BLK), i32),
            vmem((1, BLK), f32),
            vmem((n_dom, n_sub, 1, BLK), f32),
            vmem((n_dom // planes * n_sub, 1, BLK), f32),
            vmem((1, BLK), f32),
            vmem((1, BLK), f32),
            vmem((1, BLK), f32),
            vmem((n_sub, 5, capacity, BLK), f32),
            vmem((n_sub, 5, capacity, BLK), f32),
            vmem((5, RIM, BLK), f32),
            vmem((5, RIM, BLK), f32),
            vmem((padded, BLK), i32),
            vmem((padded, BLK), i32),
            vmem((padded, BLK), i32),
            vmem((padded, BLK), i32),
            vmem((RAW, padded, BLK), f32),
            vmem((PACKED, padded, BLK), i32),
            vmem((RAW, padded, BLK), f32),
            vmem((PACKED, padded, BLK), i32),
            vmem((10, padded, BLK), f32),
            vmem((5 * PIECES, padded, BLK), f32),
            sem((blocks + 30,)),
            sem((n_sub,)),
            sem((n_sub,)),
            sem((2,)),
            sem((2,)),
            sem((planes,)),
            sem((planes,)),
            sem,
            sem,
            sem((n_sub,)),
            sem((n_sub,)),
            sem,
            sem,
            pltpu.SemaphoreType.REGULAR,
            pltpu.SemaphoreType.REGULAR,
        ],
        compiler_params=pltpu.CompilerParams(collective_id=0, has_side_effects=True),
        name="hydro_step",
    )(*operands)
    spaces = (pltpu.VMEM, pltpu.VMEM, pltpu.SMEM)
    rate, new, step = (pltpu.with_memory_space_constraint(x, m) for x, m in zip((rate, new, step), spaces))
    rate, new, step = pl.pallas_call(
        finish,
        out_shape=[jax.ShapeDtypeStruct(x.shape, f32) for x in (rate, new, step)],
        in_specs=[pl.BlockSpec(memory_space=space) for space in spaces],
        out_specs=[pl.BlockSpec(memory_space=pl.ANY)] * 3,
        scratch_shapes=[sem((3,))],
        compiler_params=pltpu.CompilerParams(vmem_limit_bytes=2**20),
        name="finish",
    )(rate, new, step)
    flat = lambda x: x.transpose(1, 0, 2).reshape(5, cells)
    return flat(rate), flat(new), step.reshape(())


def solution(mesh):
    both = ("dom", "sub")
    wide, flat = P(None, both), P(both)
    in_specs = (wide, wide, flat, flat, flat, wide, flat, wide, flat, flat, wide, flat, wide, flat)
    out_specs = (wide, wide, P())
    step = functools.partial(body, (mesh.shape["dom"], mesh.shape["sub"]))
    return jax.shard_map(step, mesh=mesh, in_specs=in_specs, out_specs=out_specs, check_vma=False)
```

time: 26.4 us -> 16.9 us (0.64)
  the two profiles are of different devices: /device:TPU:0 before, /device:TPU:16 now
where the time goes in v1:
time: 16.9 us; the launch traced here: 16.7 us
  Pallas kernels  16 us (95%)
  between operations  0.64 us (4%)
    pallas_call x1, Pallas kernels, body(): pl.pallas_call(functools.partial(kernel, dims), out_shape=(vmem((blocks,...  15.4 us
    pallas_call x1, Pallas kernels, body(): pl.pallas_call(finish, out_shape=[jax.ShapeDtypeStruct(x.shape, f32) for...  0.67 us

profile of v1, /device:TPU:16, one launch (start us, length us, event | category | flops | bytes accessed | tf_op | source)
XLA Modules:
  0.0 16.7 jit_solution(16008414881115490969)
XLA Ops:
  0.6 15.4 %hydro_step.1 = (f32[16,5,128]{2,1,0:T(8,128)S(1)}, f32[16,5,128]{2,1,0:T(8,128)S(1)}, f32[1]{0:T(128)S(4)}) custom-call(s32[16]{0:T(128)} %send_hbm.1, f32[16,5,128]{2,1,0:T(8,128)} %bitcast.30, f32[15,2048]{1,0:T(8,128)} %grad_hbm.1, f32[16,128]{1,0:T(8,128)} %bitcast.36, s32[48,128]{1,0:T(8,128)} %bitcast.32, s32[48,128]{1,0:T(8,128)} %bitcast.33, ...), custom_call_target="tpu_custom_call" | custom-call | tf_op jit(solution)/shard_map/hydro_step/pallas_call | solution.py:701
  16.0 0.7 %finish.1 = (f32[16,5,128]{2,1,0:T(8,128)}, f32[16,5,128]{2,1,0:T(8,128)}, f32[1]{0:T(128)}) custom-call(f32[16,5,128]{2,1,0:T(8,128)S(1)} %get-tuple-element.9.rate, f32[16,5,128]{2,1,0:T(8,128)S(1)} %get-tuple-element.10.new, f32[1]{0:T(128)S(4)} %get-tuple-element.11.step), custom_call_target="tpu_custom_call" | custom-call | tf_op jit(solution)/shard_map/finish/pallas_call | solution.py:771

commit v2 on v1

v2 whole, which is shorter than its diff:
```python
import functools
import jax
import jax.numpy as jnp
from jax import lax
from jax.experimental import pallas as pl
from jax.experimental.pallas import tpu as pltpu
from jax.sharding import PartitionSpec as P

BLK = 128
RIM = 4
GROUP = 26
PIECES = 2
WORDS = 10
STEPS = 32767.0
PRIM_STEP = 3.0 / STEPS
GRAD_STEP = 1.5 / STEPS

adiabatic = 5.0 / 3.0
courant = 0.3
MESH = pl.DeviceIdType.MESH


def sin_cos(x):
    turns = jnp.floor(x * 0.63661977236 + 0.5)
    r = (x - turns * 1.57079637050628662109375) - turns * -4.37113900018624283e-8
    r2 = r * r
    sine = r + r * r2 * (-1.6666667163e-1 + r2 * (8.3333337680e-3 + r2 * (-1.9841270114e-4 + r2 * 2.7557314297e-6)))
    cosine = 1.0 + r2 * (-0.5 + r2 * (4.1666667908e-2 + r2 * (-1.3888889225e-3 + r2 * 2.4801587642e-5)))
    odd = jnp.abs(turns) == 1.0
    s = jnp.where(odd, cosine, sine)
    c = jnp.where(odd, sine, cosine)
    s = jnp.where((turns < 0.0) | (turns > 1.0), -s, s)
    c = jnp.where((turns > 0.0) | (turns < -1.0), -c, c)
    return s, c


def pack_pair(a, b, scale_a, scale_b):
    high = (a * scale_a + 32768.5).astype(jnp.int32)
    low = (b * scale_b + 32768.5).astype(jnp.int32)
    return lax.shift_left(high, jnp.full_like(high, 16)) + (low + jnp.int32(-(2**31)))


def pack_block(store, upper, lower, rest):
    mixed = lax.broadcasted_iota(jnp.int32, (8, BLK), 0) == 7
    scale = jnp.where(mixed, 1.0 / PRIM_STEP, 1.0 / GRAD_STEP)
    store(0, 8, pack_pair(upper, lower, 1.0 / GRAD_STEP, scale))
    store(8, 2, pack_pair(rest[0:2], rest[2:4], 1.0 / PRIM_STEP, 1.0 / PRIM_STEP))


def side_state(word, offsets):
    high, low = [], []
    for w in range(WORDS):
        value = word(w)
        high.append(lax.shift_right_arithmetic(value, jnp.full_like(value, 16)).astype(jnp.float32))
        low.append(((value & 65535) - 32768).astype(jnp.float32))
    slope = high[:8] + low[:7]
    centre = [low[7], high[8], high[9], low[8], low[9]]
    offsets = [r * GRAD_STEP for r in offsets]
    values = [centre[c] * PRIM_STEP + dot3(slope[3 * c : 3 * c + 3], offsets) for c in range(5)]
    sound = jnp.exp((values[4] - values[0]) * 0.5) * (adiabatic**0.5)
    return jnp.exp(values[0]), values[1:4], jnp.exp(values[4]), sound


def dot3(a, b):
    return a[0] * b[0] + a[1] * b[1] + a[2] * b[2]


def hllc(normal, left, right):
    dl, vl, pl_, cl, ul = left
    dr, vr, pr, cr = right
    ur = dot3(vr, normal)
    signal_l = jnp.minimum(ul - cl, ur - cr)
    signal_r = jnp.maximum(ul + cl, ur + cr)
    mass_l = dl * (signal_l - ul)
    mass_r = dr * (signal_r - ur)
    contact = (pr - pl_ + mass_l * ul - mass_r * ur) / (mass_l - mass_r)
    outer = signal_l >= 0
    from_left = jnp.logical_or(outer, contact >= 0)
    starred = jnp.where(from_left, signal_l, -signal_r) < 0
    pick = lambda a, b: jnp.where(from_left, a, b)
    density, pressure, speed, sound = pick(dl, dr), pick(pl_, pr), pick(ul, ur), pick(cl, cr)
    velocity = [pick(a, b) for a, b in zip(vl, vr)]
    signal, mass_rate = pick(signal_l, signal_r), pick(mass_l, mass_r)
    specific = sound * sound * (1.0 / (adiabatic * (adiabatic - 1.0))) + 0.5 * dot3(velocity, velocity)
    energy = density * specific
    jump = contact - speed
    factor = mass_rate / (signal - contact)
    rise = jnp.where(starred, signal * (factor - density), 0.0)
    push = jnp.where(starred, signal * factor * jump, 0.0)
    rate = density * speed
    out = [rate + rise]
    along = pressure + push
    carry = rate + rise
    for v, n in zip(velocity, normal):
        out.append(carry * v + along * n)
    out.append((energy + pressure) * speed + rise * specific + push * (contact + pressure / mass_rate))
    return out


def lane_gather(row, index):
    table = jnp.broadcast_to(row, index.shape)
    return jnp.take_along_axis(table, index, axis=1, mode="promise_in_bounds")


def flip(index, mask, size):
    out, bit = index, 1
    while bit < size:
        if mask & bit:
            out = out + bit * (1 - 2 * lax.rem(lax.div(index, bit), 2))
        bit *= 2
    return out


def kernel(
    dims,
    send_hbm,
    prim_rows,
    grad_hbm,
    volume_hbm,
    left_hbm,
    right_hbm,
    angles_hbm,
    area_hbm,
    offsets_hbm,
    rim_left_hbm,
    rim_right_hbm,
    rim_angles_hbm,
    rim_area_hbm,
    rim_offsets_hbm,
    rate_out,
    new_out,
    step_out,
    send_list,
    prim,
    cells,
    grad,
    faces,
    shape,
    load_spare,
    outgoing,
    ghosts,
    next_prim,
    next_grad,
    own_packed,
    ghost_packed,
    next_packed,
    min_own,
    mins,
    min_spare,
    min_base,
    ups,
    gback_send,
    gback_recv,
    rback_send,
    rback_recv,
    hi_left,
    lo_left,
    hi_right,
    lo_right,
    left_words,
    right_words,
    ready,
    pieces,
    load_sem,
    ghost_send_sem,
    ghost_recv_sem,
    rim_send_sem,
    rim_recv_sem,
    min_send_sem,
    min_recv_sem,
    up_send_sem,
    up_recv_sem,
    gback_send_sem,
    gback_recv_sem,
    rback_send_sem,
    rback_recv_sem,
    hello,
    hello_next,
):
    n_dom, n_sub, capacity, blocks, face_rows = dims
    rows = face_rows + RIM
    group = max(k for k in range(1, GROUP + 1) if rows % k == 0)
    ghost_blocks = n_sub * capacity
    me_dom = lax.axis_index("dom")
    me_sub = lax.axis_index("sub")
    plane = 1
    planes = n_dom // plane
    my_plane = lax.div(me_dom, plane)
    base_dom = my_plane * plane
    last = me_dom == n_dom - 1
    first = me_dom == 0
    power = n_sub & (n_sub - 1) == 0

    def to_peer(k):
        return flip(me_sub, k, n_sub) if power else lax.rem(me_sub + k, n_sub)

    def from_peer(k):
        return flip(me_sub, k, n_sub) if power else lax.rem(me_sub + n_sub - k, n_sub)

    far_first = list(range(n_sub - 1, 0, -1))
    near = [1]

    tail = pl.ds(face_rows, RIM)
    body = slice(0, face_rows)
    pairs = [(send_hbm, send_list, 0), (prim_rows, prim, 1)]
    pairs += [(grad_hbm.at[:, h * BLK : (h + 1) * BLK], grad.at[h], 1) for h in range(blocks)]
    pairs += [(prim_rows.at[:, r, :], cells.at[r], 2) for r in range(5)]
    pairs += [(volume_hbm, cells.at[5], 2)]
    middle = len(pairs)
    pairs += [(left_hbm, faces.at[0, body, :], 3), (right_hbm, faces.at[1, body, :], 3)]
    pairs += [(rim_left_hbm, faces.at[0, tail, :], 3), (rim_right_hbm, faces.at[1, tail, :], 3)]
    for where, angle, offset, size in (
        (body, angles_hbm, offsets_hbm, area_hbm),
        (tail, rim_angles_hbm, rim_offsets_hbm, rim_area_hbm),
    ):
        pairs += [(angle.at[:, r, :], shape.at[r, where, :], 4) for r in range(2)]
        pairs += [(offset.at[:, r, :], shape.at[2 + r, where, :], 4) for r in range(6)]
        pairs += [(size, shape.at[8, where, :], 4)]
    loads = [pltpu.make_async_copy(a, b, load_sem.at[k]) for a, b, k in pairs]

    def loaded(k):
        used = slice(0, rows)
        whole = (send_list, load_spare, cells, faces.at[:, used, :], shape.at[:, used, :])[k]
        pltpu.make_async_copy(whole, whole, load_sem.at[k]).wait()

    angles, offsets, area = shape.at[0:2], shape.at[2:8], shape.at[8]
    volume = cells.at[5]
    for load in loads[:middle]:
        load.start()

    barrier = pltpu.get_barrier_semaphore()
    for step in range(plane):
        dom = base_dom + lax.rem(me_dom + step, plane)
        for k in range(n_sub):
            if step or k:
                pl.semaphore_signal(barrier, inc=1, device_id=(dom, to_peer(k)), device_id_type=MESH)

    def greet(p, carry):
        for step in range(plane):
            for k in range(n_sub):
                pl.semaphore_signal(barrier, inc=1, device_id=(p * plane + step, k), device_id_type=MESH)
        return carry

    for load in loads[middle:]:
        load.start()
    lax.fori_loop(my_plane + 1, planes, greet, 0)

    loaded(0)
    loaded(1)
    for k in far_first:
        for j in range(capacity):
            block = jnp.maximum(send_list[to_peer(k) * capacity + j], 0)
            slopes, centres = grad[block], prim[block]
            outgoing[k, 8 * j : 8 * j + 8, :] = slopes[0:8]
            low = 8 * capacity + 8 * j
            outgoing[k, low : low + 7, :] = slopes[8:15]
            outgoing[k, low + 7 : low + 8, :] = centres[0:1]
            outgoing[k, 16 * capacity + 4 * j : 16 * capacity + 4 * j + 4, :] = centres[1:5]

    loaded(2)
    signal = jnp.exp((cells[4] - cells[0]) * 0.5) * (adiabatic**0.5) + jnp.sqrt(
        cells[1] * cells[1] + cells[2] * cells[2] + cells[3] * cells[3]
    )
    limit = jnp.exp(jnp.log(volume[...]) * (1.0 / 3.0)) / signal
    min_own[...] = jnp.min(limit, axis=0, keepdims=True)

    def halves(slopes, centres):
        return slopes[0:8], jnp.concatenate([slopes[8:15], centres[0:1]], 0), centres[1:5]

    for h in range(blocks):

        def store(at, size, value):
            own_packed[h, at : at + size, :] = value

        pack_block(store, *halves(grad[h], prim[h]))

    loaded(3)
    over = pl.ds(face_rows, 8)
    high = lambda x: lax.shift_right_logical(x, jnp.full_like(x, 7))
    for side, hi, lo, shift in ((0, hi_left, lo_left, blocks - RIM), (1, hi_right, lo_right, blocks + ghost_blocks)):
        faces[side, face_rows + RIM : face_rows + 8, :] = faces[side, tail, :]
        hi[body, :] = high(faces[side, body, :])
        lo[...] = faces[side] & (BLK - 1)
        hi[over, :] = high(faces[side, over, :]) + shift

    def row_of(packed):
        return lambda w: packed[w : w + 1, :]

    def gather_into(target, hi, lo, starts, sources, names, keep):
        at = [pl.ds(s, 8) for s in starts]
        index = [lo[here, :] for here in at]
        wanted = [hi[here, :] for here in at]
        match = [[w == name for name in names] for w in wanted]
        for w in range(WORDS):
            values = [target[w, here, :] for here in at] if keep else [None] * len(at)
            for n, row in enumerate(sources):
                line = row(w)
                for i in range(len(at)):
                    got = lane_gather(line, index[i])
                    values[i] = got if values[i] is None else jnp.where(match[i][n], got, values[i])
            for here, value in zip(at, values):
                target[w, here, :] = value

    width = 2 if face_rows % 16 == 0 else 1
    strides = face_rows // (8 * width)

    def gather_main(target, hi, lo, sources, names, keep, begin, end):
        def one(g, carry):
            starts = [pl.multiple_of(g * (8 * width) + 8 * i, 8) for i in range(width)]
            gather_into(target, hi, lo, starts, sources, names, keep)
            return carry

        lax.fori_loop(begin, end, one, 0)

    own = [row_of(own_packed.at[h]) for h in range(blocks)]

    def gather_left(begin, end):
        gather_main(left_words, hi_left, lo_left, own, range(blocks), False, begin, end)

    begun = jnp.where(jnp.logical_and(first, me_sub < 2), max(strides - 1, 0), 0)
    gather_left(0, begun)

    count = plane * n_sub - 1 + plane * n_sub * my_plane
    pl.semaphore_wait(barrier, count)

    def await_all(some, semaphore):
        pltpu.make_async_copy(some, some, semaphore).wait()

    def remote(src, dst, send, recv, dom, sub):
        return pltpu.make_async_remote_copy(
            src_ref=src, dst_ref=dst, send_sem=send, recv_sem=recv, device_id=(dom, sub), device_id_type=MESH
        )

    def min_copy(dom, sub, p):
        here = mins.at[me_dom, me_sub]
        return remote(min_own, here, min_send_sem, min_recv_sem.at[0 if p is None else 1], dom, sub)

    for step in range(plane):
        dom = base_dom + lax.rem(me_dom + step, plane)
        for k in range(n_sub):
            if step or k:
                min_copy(dom, to_peer(k), None).start()

    ghost_copies = {
        k: remote(
            outgoing.at[k], ghosts.at[k], ghost_send_sem, ghost_recv_sem.at[0 if k in near else 1], me_dom, to_peer(k)
        )
        for k in far_first
    }
    for k in far_first:
        ghost_copies[k].start()
    rim_copies = [
        remote(src.at[0:RIM], dst, rim_send_sem, rim_recv_sem, me_dom - 1, me_sub)
        for src, dst in ((prim, next_prim), (grad, next_grad))
    ]

    def tell(p, carry):
        for step in range(plane):
            for k in range(n_sub):
                min_copy(p * plane + step, k, p).start()
        return carry

    @pl.when(jnp.logical_not(first))
    def _():
        for copy in rim_copies:
            copy.start()

    lax.fori_loop(0, my_plane, tell, 0)

    def hail(p, carry):
        there = (lax.rem(me_dom, plane) + p * plane, me_sub)
        pl.semaphore_signal(hello, inc=1, device_id=there, device_id_type=MESH)
        return carry

    lax.fori_loop(0, my_plane, hail, 0)

    @pl.when(jnp.logical_and(lax.rem(me_dom, plane) == 0, me_dom > 0))
    def _():
        pl.semaphore_signal(hello_next, inc=1, device_id=(me_dom - 1, me_sub), device_id_type=MESH)

    gather_left(begun, strides)
    gather_into(left_words, hi_left, lo_left, [face_rows], own[blocks - RIM :], range(blocks - RIM, blocks), False)

    def pack_ghosts(k):
        for j in range(capacity):
            low, rest = 8 * capacity + 8 * j, 16 * capacity + 4 * j

            def store(at, size, value):
                ghost_packed[k, j, at : at + size, :] = value

            pack_block(
                store, ghosts[k, 8 * j : 8 * j + 8, :], ghosts[k, low : low + 8, :], ghosts[k, rest : rest + 4, :]
            )

    def ghost_pass(ks, sources, names):
        await_all(ghosts.at[min(ks) : max(ks) + 1], ghost_recv_sem.at[0 if sources else 1])
        for k in ks:
            pack_ghosts(k)
        more = [row_of(ghost_packed.at[k, j]) for k in ks for j in range(capacity)]
        called = [blocks + from_peer(k) * capacity + j for k in ks for j in range(capacity)]
        gather_main(right_words, hi_right, lo_right, sources + more, names + called, not sources, 0, strides)

    ghost_pass(near, own, list(range(blocks)))

    loaded(4)
    for r in range(9):
        shape[r, face_rows + RIM : face_rows + 8, :] = shape[r, tail, :]

    def left_step(g, carry):
        here = pl.ds(pl.multiple_of(g * 8, 8), 8)
        sin_a, cos_a = sin_cos(angles[0, here, :])
        sin_b, cos_b = sin_cos(angles[1, here, :])
        normal = [sin_a * cos_b, sin_a * sin_b, cos_a]
        density, velocity, pressure, sound = side_state(
            lambda w: left_words[w, here, :],
            [offsets[k, here, :] for k in range(3)],
        )
        values = normal + [density] + velocity + [pressure, sound, dot3(velocity, normal)]
        for k, value in enumerate(values):
            ready[k, here, :] = value
        return carry

    lax.fori_loop(0, (face_rows + 8) // 8, left_step, 0)

    def await_mins(semaphore, count):
        for p in range(planes):
            if count(p) > 0:

                @pl.when(my_plane == p)
                def _():
                    await_all(min_spare.at[0 : count(p)], semaphore)

    def up_copy(p):
        there = lax.rem(me_dom, plane) + p * plane
        return remote(min_base, ups.at[my_plane], up_send_sem, up_recv_sem, there, me_sub)

    def tell_later():
        await_all(min_spare.at[0 : plane * n_sub - 1], min_recv_sem.at[0])
        small = min_own[...]
        for step in range(1, plane * n_sub):
            dom = base_dom + lax.rem(me_dom + step // n_sub, plane)
            sub = lax.rem(me_sub + step, n_sub)
            small = jnp.minimum(small, mins[dom, sub])
        min_base[...] = small

        @pl.when(my_plane < planes - 1)
        def _():
            pl.semaphore_wait(hello, planes - 1 - my_plane)

        def one(p, carry):
            up_copy(p).start()
            return carry

        lax.fori_loop(my_plane + 1, planes, one, 0)

    ghost_pass([k for k in far_first if k not in near], [], [])

    def flux_step(g, carry):
        here = pl.ds(pl.multiple_of(g * 8, 8) if isinstance(g, jax.Array) else g * 8, 8)
        kept = [ready[k, here, :] for k in range(10)]
        right = side_state(
            lambda w: right_words[w, here, :],
            [offsets[k, here, :] for k in range(3, 6)],
        )
        flux = hllc(kept[:3], (kept[3], kept[4:7], kept[7], kept[8], kept[9]), right)
        for c in range(5):
            value = flux[c] * area[here, :]
            if not isinstance(g, jax.Array):
                value = jnp.where(last, 0.0, value)
            big = value.astype(jnp.bfloat16).astype(jnp.float32)
            pieces[c, here, :] = big
            pieces[5 + c, here, :] = value - big
        return carry

    lax.fori_loop(0, face_rows // 8, flux_step, 0)

    @pl.when(last)
    def _():
        next_prim[...] = jnp.zeros_like(next_prim)
        next_grad[...] = jnp.zeros_like(next_grad)

    @pl.when(jnp.logical_not(last))
    def _():
        await_all(load_spare.at[0:RIM], rim_recv_sem)

    for h in range(RIM):
        def store(at, size, value):
            next_packed[h, at : at + size, :] = value

        pack_block(store, *halves(next_grad[h], next_prim[h]))
    start = blocks + ghost_blocks
    gather_into(
        right_words,
        hi_right,
        lo_right,
        [face_rows],
        [row_of(next_packed.at[h]) for h in range(RIM)],
        range(start, start + RIM),
        False,
    )

    flux_step(face_rows // 8, 0)
    tell_later()

    lane_iota = lax.broadcasted_iota(jnp.int32, (BLK, BLK), 0)

    def one_hot(lo, s):
        return jnp.where(lane_iota == lo[pl.ds(s, 1), :], 1.0, 0.0).astype(jnp.bfloat16)

    def spread(hi, s, place, sign):
        match = place == hi[pl.ds(s, 1), :]
        parts = []
        for c in range(5 * PIECES):
            value = pieces[c, pl.ds(s, 1), :]
            value = value if sign > 0 else -value
            parts.append(jnp.where(match, value, 0.0))
        return jnp.concatenate(parts, 0).astype(jnp.bfloat16)

    def product(a, b):
        return lax.dot_general(a, b, (((1,), (1,)), ((), ())), preferred_element_type=jnp.float32)

    def fold(total, count):
        total = total.reshape(PIECES, 5, count, BLK)
        return total[0] + total[1]

    sent = (n_sub - 1) * capacity
    away = -(-(sent + RIM) // 8) * 8
    spot = lax.broadcasted_iota(jnp.int32, (away, BLK), 0)
    away_place = spot - sent + (blocks + ghost_blocks)
    for k in range(1, n_sub):
        lower = (k - 1) * capacity
        away_place = jnp.where(
            (spot >= lower) & (spot < lower + capacity), spot - lower + (blocks + from_peer(k) * capacity), away_place
        )
    own_place = lax.broadcasted_iota(jnp.int32, (blocks, BLK), 0)

    def away_step(i, total):
        a = jnp.concatenate([spread(hi_right, i * group + k, away_place, -1) for k in range(group)], 1)
        b = jnp.concatenate([one_hot(lo_right, i * group + k) for k in range(group)], 1)
        return total + product(a, b)

    total = lax.fori_loop(0, rows // group, away_step, jnp.zeros((5 * PIECES * away, BLK), jnp.float32))
    total = fold(total, away)
    for k in range(1, n_sub):
        gback_send[k] = total[:, (k - 1) * capacity : k * capacity, :]
    rback_send[...] = total[:, sent : sent + RIM, :]
    gback_copies = {
        k: remote(
            gback_send.at[k], gback_recv.at[k], gback_send_sem, gback_recv_sem, me_dom, from_peer(k)
        )
        for k in far_first
    }
    for k in far_first:
        gback_copies[k].start()
    rback_copy = remote(rback_send, rback_recv, rback_send_sem, rback_recv_sem, me_dom + 1, me_sub)

    @pl.when(jnp.logical_and(lax.rem(me_dom, plane) == plane - 1, jnp.logical_not(last)))
    def _():
        pl.semaphore_wait(hello_next, 1)

    @pl.when(jnp.logical_not(last))
    def _():
        rback_copy.start()

    def local_step(i, total):
        a = [spread(hi_left, i * group + k, own_place, 1) for k in range(group)]
        a += [spread(hi_right, i * group + k, own_place, -1) for k in range(group)]
        b = [one_hot(lo_left, i * group + k) for k in range(group)]
        b += [one_hot(lo_right, i * group + k) for k in range(group)]
        return total + product(jnp.concatenate(a, 1), jnp.concatenate(b, 1))

    total = lax.fori_loop(0, rows // group, local_step, jnp.zeros((5 * PIECES * blocks, BLK), jnp.float32))
    net = fold(total, blocks)

    await_mins(up_recv_sem, lambda p: p)
    await_mins(min_recv_sem.at[1], lambda p: plane * n_sub * (planes - 1 - p))

    def earlier(p, small):
        return jnp.minimum(small, ups[p])

    smallest = lax.fori_loop(0, my_plane, earlier, min_base[...])

    def later(p, small):
        for step in range(plane):
            for k in range(n_sub):
                small = jnp.minimum(small, mins[p * plane + step, k])
        return small

    smallest = lax.fori_loop(my_plane + 1, planes, later, smallest)
    time_step = courant * jnp.min(smallest, axis=1, keepdims=True)
    step_out[0] = courant * jnp.min(smallest)

    @pl.when(first)
    def _():
        rback_recv[...] = jnp.zeros_like(rback_recv)

    @pl.when(jnp.logical_not(first))
    def _():
        rback_copy.wait_recv()

    await_all(gback_recv.at[1:n_sub], gback_recv_sem)

    square = cells[1] * cells[1] + cells[2] * cells[2] + cells[3] * cells[3]
    density = jnp.exp(cells[0])
    energy = jnp.exp(cells[4]) / (adiabatic - 1.0) + 0.5 * density * square
    conserved = [density, density * cells[1], density * cells[2], density * cells[3], energy]
    inverse = -1.0 / volume[...]
    for c in range(5):
        sums = net[c]
        for h in range(RIM):
            sums = sums + jnp.where(own_place == h, rback_recv[c, h : h + 1, :], 0.0)
        for k in range(1, n_sub):
            for j in range(capacity):
                wanted = send_list[to_peer(k) * capacity + j]
                sums = sums + jnp.where(own_place == wanted, gback_recv[k, c, j : j + 1, :], 0.0)
        rate = sums * inverse
        new = conserved[c] + time_step * rate
        rate_out[:, c, :] = rate
        new_out[:, c, :] = new

    @pl.when(jnp.logical_not(first))
    def _():
        await_all(load_spare.at[0:RIM], rim_send_sem)

    @pl.when(jnp.logical_not(last))
    def _():
        rback_copy.wait_send()

    await_all(ghosts.at[1:n_sub], ghost_send_sem)
    await_all(gback_recv.at[1:n_sub], gback_send_sem)
    await_mins(min_send_sem, lambda p: plane * n_sub * (p + 1) - 1)
    await_mins(up_send_sem, lambda p: planes - 1 - p)


def finish(rate, new, step, rate_out, new_out, step_out, sems):
    pairs = ((rate, rate_out), (new, new_out), (step, step_out))
    copies = [pltpu.make_async_copy(a, b, sems.at[k]) for k, (a, b) in enumerate(pairs)]
    for copy in copies:
        copy.start()
    for copy in copies:
        copy.wait()


def by_block(x):
    return x.reshape(x.shape[0], x.shape[1] // BLK, BLK).transpose(1, 0, 2)


def body(mesh_sizes, *args):
    (primitive, gradient, volume, face_left, face_right, face_angles, face_area, face_offsets) = args[:8]
    (rim_left, rim_right, rim_angles, rim_area, rim_offsets, send_list) = args[8:]
    n_dom, n_sub = mesh_sizes
    cells = primitive.shape[1]
    blocks = cells // BLK
    face_rows = face_left.shape[0] // BLK
    capacity = send_list.shape[0] // n_sub
    padded = face_rows + 8
    dims = (n_dom, n_sub, capacity, blocks, face_rows)
    f32, i32 = jnp.float32, jnp.int32
    planes = n_dom
    away = -(-((n_sub - 1) * capacity + RIM) // 8) * 8
    sem = pltpu.SemaphoreType.DMA
    operands = (
        send_list,
        by_block(primitive),
        gradient,
        volume.reshape(blocks, BLK),
        face_left.reshape(face_rows, BLK),
        face_right.reshape(face_rows, BLK),
        by_block(face_angles),
        face_area.reshape(face_rows, BLK),
        by_block(face_offsets),
        rim_left.reshape(RIM, BLK),
        rim_right.reshape(RIM, BLK),
        by_block(rim_angles),
        rim_area.reshape(RIM, BLK),
        by_block(rim_offsets),
    )
    vmem = pltpu.VMEM
    rate, new, step = pl.pallas_call(
        functools.partial(kernel, dims),
        out_shape=(
            vmem((blocks, 5, BLK), f32),
            vmem((blocks, 5, BLK), f32),
            pltpu.SMEM((1,), f32),
        ),
        in_specs=[pl.BlockSpec(memory_space=pl.ANY)] * len(operands),
        out_specs=(pl.BlockSpec(memory_space=pltpu.VMEM), pl.BlockSpec(memory_space=pltpu.VMEM), pl.BlockSpec(memory_space=pltpu.SMEM)),
        scratch_shapes=[
            pltpu.SMEM(send_list.shape, i32),
            vmem((blocks, 5, BLK), f32),
            vmem((6, blocks, BLK), f32),
            vmem((blocks, 15, BLK), f32),
            vmem((2, padded, BLK), i32),
            vmem((9, padded, BLK), f32),
            vmem((blocks, 20, BLK), f32),
            vmem((n_sub, 20 * capacity, BLK), f32),
            vmem((n_sub, 20 * capacity, BLK), f32),
            vmem((RIM, 5, BLK), f32),
            vmem((RIM, 15, BLK), f32),
            vmem((blocks, 16, BLK), i32),
            vmem((n_sub, capacity, 16, BLK), i32),
            vmem((RIM, 16, BLK), i32),
            vmem((1, BLK), f32),
            vmem((n_dom, n_sub, 1, BLK), f32),
            vmem((n_dom * n_sub, 1, BLK), f32),
            vmem((1, BLK), f32),
            vmem((planes, 1, BLK), f32),
            vmem((n_sub, 5, capacity, BLK), f32),
            vmem((n_sub, 5, capacity, BLK), f32),
            vmem((5, RIM, BLK), f32),
            vmem((5, RIM, BLK), f32),
            vmem((padded, BLK), i32),
            vmem((padded, BLK), i32),
            vmem((padded, BLK), i32),
            vmem((padded, BLK), i32),
            vmem((WORDS, padded, BLK), i32),
            vmem((WORDS, padded, BLK), i32),
            vmem((10, padded, BLK), f32),
            vmem((5 * PIECES, padded, BLK), f32),
            sem((5,)),
            sem,
            sem((2,)),
            sem,
            sem,
            sem,
            sem((2,)),
            sem,
            sem,
            sem,
            sem,
            sem,
            sem,
            pltpu.SemaphoreType.REGULAR,
            pltpu.SemaphoreType.REGULAR,
        ],
        compiler_params=pltpu.CompilerParams(collective_id=0, has_side_effects=True),
        name="hydro_step",
    )(*operands)
    spaces = (pltpu.VMEM, pltpu.VMEM, pltpu.SMEM)
    rate, new, step = (pltpu.with_memory_space_constraint(x, m) for x, m in zip((rate, new, step), spaces))
    rate, new, step = pl.pallas_call(
        finish,
        out_shape=[jax.ShapeDtypeStruct(x.shape, f32) for x in (rate, new, step)],
        in_specs=[pl.BlockSpec(memory_space=space) for space in spaces],
        out_specs=[pl.BlockSpec(memory_space=pl.ANY)] * 3,
        scratch_shapes=[sem((3,))],
        compiler_params=pltpu.CompilerParams(vmem_limit_bytes=2**20),
        name="finish",
    )(rate, new, step)
    flat = lambda x: x.transpose(1, 0, 2).reshape(5, cells)
    return flat(rate), flat(new), step.reshape(())


def solution(mesh):
    both = ("dom", "sub")
    wide, flat = P(None, both), P(both)
    in_specs = (wide, wide, flat, flat, flat, wide, flat, wide, flat, flat, wide, flat, wide, flat)
    out_specs = (wide, wide, P())
    step = functools.partial(body, (mesh.shape["dom"], mesh.shape["sub"]))
    return jax.shard_map(step, mesh=mesh, in_specs=in_specs, out_specs=out_specs, check_vma=False)
```

time: 16.9 us -> 13.7 us (0.81)
  the two profiles are of different devices: /device:TPU:16 before, /device:TPU:0 now
where the time goes in v2:
time: 13.7 us; the launch traced here: 13.5 us
  Pallas kernels  12.9 us (94%)
  between operations  0.64 us (5%)
    pallas_call x1, Pallas kernels, body(): pl.pallas_call(functools.partial(kernel, dims), out_shape=(vmem((blocks,...  12.2 us
    pallas_call x1, Pallas kernels, body(): pl.pallas_call(finish, out_shape=[jax.ShapeDtypeStruct(x.shape, f32) for...  0.67 us

profile of v2, /device:TPU:0, one launch (start us, length us, event | category | flops | bytes accessed | tf_op | source)
XLA Modules:
  0.0 13.5 jit_solution(9789403135366178622)
XLA Ops:
  0.6 12.2 %hydro_step.1 = (f32[16,5,128]{2,1,0:T(8,128)S(1)}, f32[16,5,128]{2,1,0:T(8,128)S(1)}, f32[1]{0:T(128)S(4)}) custom-call(s32[16]{0:T(128)} %send_hbm.1, f32[16,5,128]{2,1,0:T(8,128)} %bitcast.30, f32[15,2048]{1,0:T(8,128)} %grad_hbm.1, f32[16,128]{1,0:T(8,128)} %bitcast.36, s32[48,128]{1,0:T(8,128)} %bitcast.32, s32[48,128]{1,0:T(8,128)} %bitcast.33, ...), custom_call_target="tpu_custom_call" | custom-call | tf_op jit(solution)/shard_map/hydro_step/pallas_call | solution.py:679
  12.9 0.7 %finish.1 = (f32[16,5,128]{2,1,0:T(8,128)}, f32[16,5,128]{2,1,0:T(8,128)}, f32[1]{0:T(128)}) custom-call(f32[16,5,128]{2,1,0:T(8,128)S(1)} %get-tuple-element.9.rate, f32[16,5,128]{2,1,0:T(8,128)S(1)} %get-tuple-element.10.new, f32[1]{0:T(128)S(4)} %get-tuple-element.11.step), custom_call_target="tpu_custom_call" | custom-call | tf_op jit(solution)/shard_map/finish/pallas_call | solution.py:741

commit v3 on v2

--- a/solution.py
+++ b/solution.py
@@ -392,15 +392,16 @@
                 store, ghosts[k, 8 * j : 8 * j + 8, :], ghosts[k, low : low + 8, :], ghosts[k, rest : rest + 4, :]
             )
 
-    def ghost_pass(ks, sources, names):
-        await_all(ghosts.at[min(ks) : max(ks) + 1], ghost_recv_sem.at[0 if sources else 1])
+    def arrived(ks, semaphore):
+        await_all(ghosts.at[min(ks) : max(ks) + 1], semaphore)
         for k in ks:
             pack_ghosts(k)
-        more = [row_of(ghost_packed.at[k, j]) for k in ks for j in range(capacity)]
-        called = [blocks + from_peer(k) * capacity + j for k in ks for j in range(capacity)]
-        gather_main(right_words, hi_right, lo_right, sources + more, names + called, not sources, 0, strides)
-
-    ghost_pass(near, own, list(range(blocks)))
+        lines = [row_of(ghost_packed.at[k, j]) for k in ks for j in range(capacity)]
+        return lines, [blocks + from_peer(k) * capacity + j for k in ks for j in range(capacity)]
+
+    more, called = arrived(near, ghost_recv_sem.at[0])
+    sources, names = own + more, list(range(blocks)) + called
+    gather_main(right_words, hi_right, lo_right, sources, names, False, 0, strides)
 
     loaded(4)
     for r in range(9):
@@ -422,41 +423,23 @@
 
     lax.fori_loop(0, (face_rows + 8) // 8, left_step, 0)
 
-    def await_mins(semaphore, count):
-        for p in range(planes):
-            if count(p) > 0:
-
-                @pl.when(my_plane == p)
-                def _():
-                    await_all(min_spare.at[0 : count(p)], semaphore)
-
-    def up_copy(p):
-        there = lax.rem(me_dom, plane) + p * plane
-        return remote(min_base, ups.at[my_plane], up_send_sem, up_recv_sem, there, me_sub)
-
-    def tell_later():
-        await_all(min_spare.at[0 : plane * n_sub - 1], min_recv_sem.at[0])
-        small = min_own[...]
-        for step in range(1, plane * n_sub):
-            dom = base_dom + lax.rem(me_dom + step // n_sub, plane)
-            sub = lax.rem(me_sub + step, n_sub)
-            small = jnp.minimum(small, mins[dom, sub])
-        min_base[...] = small
-
-        @pl.when(my_plane < planes - 1)
-        def _():
-            pl.semaphore_wait(hello, planes - 1 - my_plane)
-
-        def one(p, carry):
-            up_copy(p).start()
-            return carry
-
-        lax.fori_loop(my_plane + 1, planes, one, 0)
-
-    ghost_pass([k for k in far_first if k not in near], [], [])
-
-    def flux_step(g, carry):
-        here = pl.ds(pl.multiple_of(g * 8, 8) if isinstance(g, jax.Array) else g * 8, 8)
+
+    @pl.when(last)
+    def _():
+        next_prim[...] = jnp.zeros_like(next_prim)
+        next_grad[...] = jnp.zeros_like(next_grad)
+
+    @pl.when(jnp.logical_not(last))
+    def _():
+        await_all(load_spare.at[0:RIM], rim_recv_sem)
+
+    for h in range(RIM):
+        def store(at, size, value):
+            next_packed[h, at : at + size, :] = value
+
+        pack_block(store, *halves(next_grad[h], next_prim[h]))
+    def flux_step(g):
+        here = pl.ds(g * 8, 8)
         kept = [ready[k, here, :] for k in range(10)]
         right = side_state(
             lambda w: right_words[w, here, :],
@@ -465,42 +448,11 @@
         flux = hllc(kept[:3], (kept[3], kept[4:7], kept[7], kept[8], kept[9]), right)
         for c in range(5):
             value = flux[c] * area[here, :]
-            if not isinstance(g, jax.Array):
+            if g * 8 >= face_rows:
                 value = jnp.where(last, 0.0, value)
             big = value.astype(jnp.bfloat16).astype(jnp.float32)
             pieces[c, here, :] = big
             pieces[5 + c, here, :] = value - big
-        return carry
-
-    lax.fori_loop(0, face_rows // 8, flux_step, 0)
-
-    @pl.when(last)
-    def _():
-        next_prim[...] = jnp.zeros_like(next_prim)
-        next_grad[...] = jnp.zeros_like(next_grad)
-
-    @pl.when(jnp.logical_not(last))
-    def _():
-        await_all(load_spare.at[0:RIM], rim_recv_sem)
-
-    for h in range(RIM):
-        def store(at, size, value):
-            next_packed[h, at : at + size, :] = value
-
-        pack_block(store, *halves(next_grad[h], next_prim[h]))
-    start = blocks + ghost_blocks
-    gather_into(
-        right_words,
-        hi_right,
-        lo_right,
-        [face_rows],
-        [row_of(next_packed.at[h]) for h in range(RIM)],
-        range(start, start + RIM),
-        False,
-    )
-
-    flux_step(face_rows // 8, 0)
-    tell_later()
 
     lane_iota = lax.broadcasted_iota(jnp.int32, (BLK, BLK), 0)
 
@@ -534,12 +486,40 @@
         )
     own_place = lax.broadcasted_iota(jnp.int32, (blocks, BLK), 0)
 
-    def away_step(i, total):
-        a = jnp.concatenate([spread(hi_right, i * group + k, away_place, -1) for k in range(group)], 1)
-        b = jnp.concatenate([one_hot(lo_right, i * group + k) for k in range(group)], 1)
-        return total + product(a, b)
-
-    total = lax.fori_loop(0, rows // group, away_step, jnp.zeros((5 * PIECES * away, BLK), jnp.float32))
+    def away_rows(which):
+        a = jnp.concatenate([spread(hi_right, s, away_place, -1) for s in which], 1)
+        b = jnp.concatenate([one_hot(lo_right, s) for s in which], 1)
+        return product(a, b)
+
+    def rim_rows():
+        start = blocks + ghost_blocks
+        gather_into(
+            right_words,
+            hi_right,
+            lo_right,
+            [face_rows],
+            [row_of(next_packed.at[h]) for h in range(RIM)],
+            range(start, start + RIM),
+            False,
+        )
+
+
+    lines, called = arrived([k for k in far_first if k not in near], ghost_recv_sem.at[1])
+    total = jnp.zeros((5 * PIECES * away, BLK), jnp.float32)
+    span = 8 * width
+    for t in range(strides + 2):
+        if t < strides:
+            at = [t * span + 8 * i for i in range(width)]
+            gather_into(right_words, hi_right, lo_right, at, lines, called, True)
+        if t == strides - 1:
+            rim_rows()
+        if 1 <= t <= strides:
+            for i in range(width):
+                flux_step((t - 1) * width + i)
+        if t == strides:
+            flux_step(face_rows // 8)
+        if t >= 2:
+            total = total + away_rows(range((t - 2) * span, (t - 1) * span + (RIM if t == strides + 1 else 0)))
     total = fold(total, away)
     for k in range(1, n_sub):
         gback_send[k] = total[:, (k - 1) * capacity : k * capacity, :]
@@ -561,6 +541,39 @@
     @pl.when(jnp.logical_not(last))
     def _():
         rback_copy.start()
+
+    def await_mins(semaphore, count):
+        for p in range(planes):
+            if count(p) > 0:
+
+                @pl.when(my_plane == p)
+                def _():
+                    await_all(min_spare.at[0 : count(p)], semaphore)
+
+    def up_copy(p):
+        there = lax.rem(me_dom, plane) + p * plane
+        return remote(min_base, ups.at[my_plane], up_send_sem, up_recv_sem, there, me_sub)
+
+    def tell_later():
+        await_all(min_spare.at[0 : plane * n_sub - 1], min_recv_sem.at[0])
+        small = min_own[...]
+        for step in range(1, plane * n_sub):
+            dom = base_dom + lax.rem(me_dom + step // n_sub, plane)
+            sub = lax.rem(me_sub + step, n_sub)
+            small = jnp.minimum(small, mins[dom, sub])
+        min_base[...] = small
+
+        @pl.when(my_plane < planes - 1)
+        def _():
+            pl.semaphore_wait(hello, planes - 1 - my_plane)
+
+        def one(p, carry):
+            up_copy(p).start()
+            return carry
+
+        lax.fori_loop(my_plane + 1, planes, one, 0)
+
+    tell_later()
 
     def local_step(i, total):
         a = [spread(hi_left, i * group + k, own_place, 1) for k in range(group)]

time: 13.7 us -> 12.7 us (0.927)
  Pallas kernels: 12.9 us -> 11.9 us
    pallas_call x1, Pallas kernels: 12.2 us -> 11.2 us  [body(): pl.pallas_call(functools.partial(kernel, dims), out_shape=(vmem((blocks,...]
where the time goes in v3:
time: 12.7 us; the launch traced here: 12.5 us
  Pallas kernels  11.9 us (94%)
  between operations  0.64 us (5%)
    pallas_call x1, Pallas kernels, body(): pl.pallas_call(functools.partial(kernel, dims), out_shape=(vmem((blocks,...  11.2 us
    pallas_call x1, Pallas kernels, body(): pl.pallas_call(finish, out_shape=[jax.ShapeDtypeStruct(x.shape, f32) for...  0.67 us

profile of v3, /device:TPU:0, one launch (start us, length us, event | category | flops | bytes accessed | tf_op | source)
XLA Modules:
  0.0 12.5 jit_solution(18084577490829864364)
XLA Ops:
  0.6 11.2 %hydro_step.1 = (f32[16,5,128]{2,1,0:T(8,128)S(1)}, f32[16,5,128]{2,1,0:T(8,128)S(1)}, f32[1]{0:T(128)S(4)}) custom-call(s32[16]{0:T(128)} %send_hbm.1, f32[16,5,128]{2,1,0:T(8,128)} %bitcast.30, f32[15,2048]{1,0:T(8,128)} %grad_hbm.1, f32[16,128]{1,0:T(8,128)} %bitcast.36, s32[48,128]{1,0:T(8,128)} %bitcast.32, s32[48,128]{1,0:T(8,128)} %bitcast.33, ...), custom_call_target="tpu_custom_call" | custom-call | tf_op jit(solution)/shard_map/hydro_step/pallas_call | solution.py:692
  11.9 0.7 %finish.1 = (f32[16,5,128]{2,1,0:T(8,128)}, f32[16,5,128]{2,1,0:T(8,128)}, f32[1]{0:T(128)}) custom-call(f32[16,5,128]{2,1,0:T(8,128)S(1)} %get-tuple-element.9.rate, f32[16,5,128]{2,1,0:T(8,128)S(1)} %get-tuple-element.10.new, f32[1]{0:T(128)S(4)} %get-tuple-element.11.step), custom_call_target="tpu_custom_call" | custom-call | tf_op jit(solution)/shard_map/finish/pallas_call | solution.py:754

commit v4 on v3

--- a/solution.py
+++ b/solution.py
@@ -199,6 +199,16 @@
 
     far_first = list(range(n_sub - 1, 0, -1))
     near = [1]
+    parity = lax.rem(me_sub, 2)
+
+    def send_order():
+        if not power:
+            return [(k, to_peer(k), from_peer(k)) for k in far_first]
+        order = []
+        for m in range(n_sub - 2, 0, -2):
+            even = flip(me_sub, m, n_sub) - parity
+            order += [(m + parity, even, even), (m + 1 - parity, even + 1, even + 1)]
+        return order + [(1, to_peer(1), from_peer(1))]
 
     tail = pl.ds(face_rows, RIM)
     body = slice(0, face_rows)
@@ -341,14 +351,9 @@
             if step or k:
                 min_copy(dom, to_peer(k), None).start()
 
-    ghost_copies = {
-        k: remote(
-            outgoing.at[k], ghosts.at[k], ghost_send_sem, ghost_recv_sem.at[0 if k in near else 1], me_dom, to_peer(k)
-        )
-        for k in far_first
-    }
-    for k in far_first:
-        ghost_copies[k].start()
+    for k, peer, _ in send_order():
+        arrival = ghost_recv_sem.at[0 if isinstance(k, int) and k in near else 1]
+        remote(outgoing.at[k], ghosts.at[k], ghost_send_sem, arrival, me_dom, peer).start()
     rim_copies = [
         remote(src.at[0:RIM], dst, rim_send_sem, rim_recv_sem, me_dom - 1, me_sub)
         for src, dst in ((prim, next_prim), (grad, next_grad))
@@ -424,20 +429,6 @@
     lax.fori_loop(0, (face_rows + 8) // 8, left_step, 0)
 
 
-    @pl.when(last)
-    def _():
-        next_prim[...] = jnp.zeros_like(next_prim)
-        next_grad[...] = jnp.zeros_like(next_grad)
-
-    @pl.when(jnp.logical_not(last))
-    def _():
-        await_all(load_spare.at[0:RIM], rim_recv_sem)
-
-    for h in range(RIM):
-        def store(at, size, value):
-            next_packed[h, at : at + size, :] = value
-
-        pack_block(store, *halves(next_grad[h], next_prim[h]))
     def flux_step(g):
         here = pl.ds(g * 8, 8)
         kept = [ready[k, here, :] for k in range(10)]
@@ -476,9 +467,9 @@
         return total[0] + total[1]
 
     sent = (n_sub - 1) * capacity
-    away = -(-(sent + RIM) // 8) * 8
+    away = -(-sent // 8) * 8
     spot = lax.broadcasted_iota(jnp.int32, (away, BLK), 0)
-    away_place = spot - sent + (blocks + ghost_blocks)
+    away_place = jnp.full_like(spot, -1)
     for k in range(1, n_sub):
         lower = (k - 1) * capacity
         away_place = jnp.where(
@@ -486,11 +477,42 @@
         )
     own_place = lax.broadcasted_iota(jnp.int32, (blocks, BLK), 0)
 
-    def away_rows(which):
-        a = jnp.concatenate([spread(hi_right, s, away_place, -1) for s in which], 1)
+    def away_rows(which, place):
+        a = jnp.concatenate([spread(hi_right, s, place, -1) for s in which], 1)
         b = jnp.concatenate([one_hot(lo_right, s) for s in which], 1)
         return product(a, b)
 
+    lines, called = arrived([k for k in far_first if k not in near], ghost_recv_sem.at[1])
+    total = jnp.zeros((5 * PIECES * away, BLK), jnp.float32)
+    span = 8 * width
+    for t in range(strides + 2):
+        if t < strides:
+            at = [t * span + 8 * i for i in range(width)]
+            gather_into(right_words, hi_right, lo_right, at, lines, called, True)
+        if 1 <= t <= strides:
+            for i in range(width):
+                flux_step((t - 1) * width + i)
+        if t >= 2:
+            total = total + away_rows(range((t - 2) * span, (t - 1) * span), away_place)
+    total = fold(total, away)
+    for k in range(1, n_sub):
+        gback_send[k] = total[:, (k - 1) * capacity : k * capacity, :]
+    for k, _, peer in send_order():
+        remote(gback_send.at[k], gback_recv.at[k], gback_send_sem, gback_recv_sem, me_dom, peer).start()
+    @pl.when(last)
+    def _():
+        next_prim[...] = jnp.zeros_like(next_prim)
+        next_grad[...] = jnp.zeros_like(next_grad)
+
+    @pl.when(jnp.logical_not(last))
+    def _():
+        await_all(load_spare.at[0:RIM], rim_recv_sem)
+
+    for h in range(RIM):
+        def store(at, size, value):
+            next_packed[h, at : at + size, :] = value
+
+        pack_block(store, *halves(next_grad[h], next_prim[h]))
     def rim_rows():
         start = blocks + ghost_blocks
         gather_into(
@@ -504,34 +526,11 @@
         )
 
 
-    lines, called = arrived([k for k in far_first if k not in near], ghost_recv_sem.at[1])
-    total = jnp.zeros((5 * PIECES * away, BLK), jnp.float32)
-    span = 8 * width
-    for t in range(strides + 2):
-        if t < strides:
-            at = [t * span + 8 * i for i in range(width)]
-            gather_into(right_words, hi_right, lo_right, at, lines, called, True)
-        if t == strides - 1:
-            rim_rows()
-        if 1 <= t <= strides:
-            for i in range(width):
-                flux_step((t - 1) * width + i)
-        if t == strides:
-            flux_step(face_rows // 8)
-        if t >= 2:
-            total = total + away_rows(range((t - 2) * span, (t - 1) * span + (RIM if t == strides + 1 else 0)))
-    total = fold(total, away)
-    for k in range(1, n_sub):
-        gback_send[k] = total[:, (k - 1) * capacity : k * capacity, :]
-    rback_send[...] = total[:, sent : sent + RIM, :]
-    gback_copies = {
-        k: remote(
-            gback_send.at[k], gback_recv.at[k], gback_send_sem, gback_recv_sem, me_dom, from_peer(k)
-        )
-        for k in far_first
-    }
-    for k in far_first:
-        gback_copies[k].start()
+    rim_rows()
+    flux_step(face_rows // 8)
+    rim_place = lax.broadcasted_iota(jnp.int32, (8, BLK), 0) + (blocks + ghost_blocks)
+    total = fold(away_rows(range(face_rows, rows), rim_place), 8)
+    rback_send[...] = total[:, 0:RIM, :]
     rback_copy = remote(rback_send, rback_recv, rback_send_sem, rback_recv_sem, me_dom + 1, me_sub)
 
     @pl.when(jnp.logical_and(lax.rem(me_dom, plane) == plane - 1, jnp.logical_not(last)))
@@ -670,7 +669,6 @@
     dims = (n_dom, n_sub, capacity, blocks, face_rows)
     f32, i32 = jnp.float32, jnp.int32
     planes = n_dom
-    away = -(-((n_sub - 1) * capacity + RIM) // 8) * 8
     sem = pltpu.SemaphoreType.DMA
     operands = (
         send_list,

time: 12.7 us -> 12.2 us (0.961)
  Pallas kernels: 11.9 us -> 11.3 us
    pallas_call x1, Pallas kernels: 11.2 us -> 10.6 us  [body(): pl.pallas_call(functools.partial(kernel, dims), out_shape=(vmem((blocks,...]
where the time goes in v4:
time: 12.2 us; the launch traced here: 12 us
  Pallas kernels  11.3 us (93%)
  between operations  0.64 us (5%)
    pallas_call x1, Pallas kernels, body(): pl.pallas_call(functools.partial(kernel, dims), out_shape=(vmem((blocks,...  10.6 us
    pallas_call x1, Pallas kernels, body(): pl.pallas_call(finish, out_shape=[jax.ShapeDtypeStruct(x.shape, f32) for...  0.67 us

profile of v4, /device:TPU:0, one launch (start us, length us, event | category | flops | bytes accessed | tf_op | source)
XLA Modules:
  0.0 12.0 jit_solution(12114440203659980072)
XLA Ops:
  0.6 10.6 %hydro_step.1 = (f32[16,5,128]{2,1,0:T(8,128)S(1)}, f32[16,5,128]{2,1,0:T(8,128)S(1)}, f32[1]{0:T(128)S(4)}) custom-call(s32[16]{0:T(128)} %send_hbm.1, f32[16,5,128]{2,1,0:T(8,128)} %bitcast.30, f32[15,2048]{1,0:T(8,128)} %grad_hbm.1, f32[16,128]{1,0:T(8,128)} %bitcast.36, s32[48,128]{1,0:T(8,128)} %bitcast.32, s32[48,128]{1,0:T(8,128)} %bitcast.33, ...), custom_call_target="tpu_custom_call" | custom-call | tf_op jit(solution)/shard_map/hydro_step/pallas_call | solution.py:690
  11.3 0.7 %finish.1 = (f32[16,5,128]{2,1,0:T(8,128)}, f32[16,5,128]{2,1,0:T(8,128)}, f32[1]{0:T(128)}) custom-call(f32[16,5,128]{2,1,0:T(8,128)S(1)} %get-tuple-element.9.rate, f32[16,5,128]{2,1,0:T(8,128)S(1)} %get-tuple-element.10.new, f32[1]{0:T(128)S(4)} %get-tuple-element.11.step), custom_call_target="tpu_custom_call" | custom-call | tf_op jit(solution)/shard_map/finish/pallas_call | solution.py:752
